TPU v7x, 256 devices: a 8x8x2 block of a 8x8x16 slice. The times are simulated.
256 devices in a mesh: sweep: 2 (over z), expert: 16 (over y, core), fsdp: 8 (over x).
Axes of the slice: x: 8, y: 8, z: 2, core: 2. Of those that a mesh axis runs over, the one named last changes fastest.
The devices are a block of a 8x8x16 slice.
Arguments:
- tokens: bfloat16 [32768, 2048], P(('sweep', 'expert', 'fsdp')), parts along dimension 0, may hold values from -6 to 6
- context: bfloat16 [32768, 2048], P(('sweep', 'expert', 'fsdp')), parts along dimension 0, may hold values from -6 to 6
- out_proj: bfloat16 [4096, 2048], P(('sweep', 'expert', 'fsdp')), parts along dimension 0, may hold values from -0.125 to 0.125
- norm_gain: float32 [4096], P('sweep'), parts along dimension 0, may hold values from 0.1 to 1.9
- router: bfloat16 [4096, 64], P('sweep'), parts along dimension 0, may hold values from -0.125 to 0.125
- expert_ids: int32 [32768, 2], P(('sweep', 'expert', 'fsdp')), parts along dimension 0, may hold values from 0 to 63, all different within a row; in each aligned block of 128 rows (0 to 127, 128 to 255, ...) at most 5 rows name the same one
- w_gate_up: bfloat16 [256, 2, 704, 2048], P(('sweep', 'expert', 'fsdp')), parts along dimension 0, may hold values from -0.125 to 0.125
- w_down: bfloat16 [256, 704, 2048], P(('sweep', 'expert', 'fsdp')), parts along dimension 0, may hold values from -0.15625 to 0.15625
Outputs:
- layer_out: bfloat16 [32768, 2048], P(('sweep', 'expert', 'fsdp')), parts along dimension 0
There are 2 independent parts, one for each index of `sweep`. A program takes and returns all parts, laid end to end along the dimension named above; each array names one. Nothing has to cross between parts.
Inputs may be any that keep to these rules, and one draw needn't show every extreme that they name: `expert_ids`: each row names two different experts. Among the rows of one device no expert is named more than 5 times, a bound that some block reaches.
All inputs are finite; a program needn't handle non-finite values.
Results may differ from a plain program's by a relative error of at most 0.012.
Values may be sent and summed in bfloat16 or wider, within the bound.
No kernel may reach another device: no remote copies, remote signals or barrier semaphores. Data moves between devices by JAX's collectives and lax.ppermute only.
A program may use at most 64 MiB of HBM per device.

v0:
```python
import jax
import jax.numpy as jnp
from jax import lax
from jax.sharding import PartitionSpec as P

eps_norm = 1e-05


def half_block(taken, gate_up_w, down_w):
    gate_up = jnp.einsum("rd,kfd->krf", taken, gate_up_w, preferred_element_type=jnp.float32)
    hidden = (jax.nn.silu(gate_up[0]) * gate_up[1]).astype(jnp.bfloat16)
    return jnp.dot(hidden, down_w, preferred_element_type=jnp.float32).astype(jnp.bfloat16)


def slot_places(expert_ids, experts):
    flat_ids = expert_ids.reshape(-1)
    onehot = (flat_ids[:, None] == jnp.arange(experts, dtype=jnp.int32)[None, :]).astype(jnp.int32)
    before = jnp.cumsum(onehot, axis=0) - onehot
    places = jnp.sum(before * onehot, axis=1)
    return (flat_ids, places)


def on_device(tokens, context, out_proj, norm_gain, router, expert_ids, w_gate_up, w_down):
    rows_here, width = tokens.shape
    columns = lax.axis_size("expert")
    members = lax.axis_size("fsdp")
    experts = columns * members // 2
    group = members // 2
    slot_cap = 5 * rows_here // (2 * experts)
    gate_up_here = w_gate_up[0]
    down_here = w_down[0]
    attended = jnp.dot(
        context,
        lax.all_gather(out_proj, ("expert", "fsdp"), axis=0, tiled=True),
        preferred_element_type=jnp.float32,
    )
    residual_in = (tokens.astype(jnp.float32) + attended).astype(jnp.bfloat16)
    widened = residual_in.astype(jnp.float32)
    inv_rms = lax.rsqrt(jnp.mean(widened * widened, axis=1, keepdims=True) + eps_norm)
    normed = (widened * inv_rms * norm_gain).astype(jnp.bfloat16)
    logits = jnp.dot(normed, router, preferred_element_type=jnp.float32)
    picked = jnp.take_along_axis(logits, expert_ids, axis=1)
    scores = jax.nn.sigmoid(picked)
    gate_vals = scores / jnp.sum(scores, axis=1, keepdims=True)
    flat_ids, places = slot_places(expert_ids, experts)
    source_rows = jnp.repeat(normed, 2, axis=0)
    empty_box = jnp.zeros((experts * slot_cap, width), jnp.bfloat16)
    target = (flat_ids % group * columns + flat_ids // group) * slot_cap + places
    outbox = empty_box.at[target].set(source_rows).reshape(group, columns, slot_cap, width)
    arrived = lax.all_to_all(outbox, "expert", split_axis=1, concat_axis=1, tiled=True)
    copies = jnp.repeat(arrived, 2, axis=0)
    pieces = lax.all_to_all(copies, "fsdp", split_axis=0, concat_axis=0, tiled=True)
    slots_in = pieces.shape[2]
    output_half = half_block(
        pieces.reshape(members * columns * slots_in, width), gate_up_here, down_here
    )
    partials = output_half.reshape(members, columns, slots_in, width)
    back = lax.all_to_all(partials, "fsdp", split_axis=0, concat_axis=0, tiled=True)
    halves = back.reshape(group, 2, columns, slot_cap, width).astype(jnp.float32)
    summed = (halves[:, 0] + halves[:, 1]).astype(jnp.bfloat16)
    finished = lax.all_to_all(summed, "expert", split_axis=1, concat_axis=1, tiled=True)
    results = finished.reshape(-1, width)[target].astype(jnp.float32).reshape(rows_here, 2, width)
    output_rows = widened + gate_vals[:, 0:1] * results[:, 0] + gate_vals[:, 1:2] * results[:, 1]
    return output_rows.astype(jnp.bfloat16)


def solution(mesh):
    return jax.shard_map(
        on_device,
        mesh=mesh,
        in_specs=(
            P(("sweep", "expert", "fsdp"), None),
            P(("sweep", "expert", "fsdp"), None),
            P(("sweep", "expert", "fsdp"), None),
            P("sweep"),
            P("sweep", None),
            P(("sweep", "expert", "fsdp"), None),
            P(("sweep", "expert", "fsdp"), None, None, None),
            P(("sweep", "expert", "fsdp"), None, None),
        ),
        out_specs=P(("sweep", "expert", "fsdp"), None),
        check_vma=False,
    )
```

profile of v0, /device:TPU:513, one launch (start us, length us, event | category | flops | bytes accessed | tf_op | source)
XLA Modules:
  0.0 400.5 jit_solution(119510280563451889)
XLA Ops:
  6.6 0.7 all-gather.2.cloned.1.call-update
  7.3 0.9 copy.57
  8.6 0.6 reduce-window.6
  9.6 103.9 %all-gather.2.cloned.1.call-done = bf16[2048,2048]{1,0:T(8,128)(2,1)} async-done(((bf16[16,2048]{1,0:T(8,128)(2,1)}), bf16[2048,2048]{1,0:T(8,128)(2,1)}) %all-gather.2.cloned.1.call-update) | async-done | bytes 8388624 | tf_op jit(solution)/shard_map/all_gather | solution.py:34
  113.6 5.0 %multiply_reduce_fusion = (f32[128]{0:T(128)S(1)}, f32[128,2048]{1,0:T(8,128)S(1)}) fusion(bf16[128,2048]{1,0:T(8,128)(2,1)} %param.9, bf16[2048,2048]{1,0:T(8,128)(2,1)} %all-gather.2.cloned.1.call-done, bf16[128,2048]{1,0:T(8,128)(2,1)} %param.8), kind=kOutput, calls=%fused_computation.24 | convolution fusion | flops 1075314560 | bytes 10486272 | tf_op jit(solution)/shard_map/dot_general | solution.py:32
  118.6 1.0 copy-done.2
  119.7 1.7 broadcast_in_dim.21
  121.3 2.3 reshape.216
  123.6 4.0 scatter_custom_fusion
  127.6 3.4 reshape.191
  131.0 2.9 copy.61
  133.8 39.0 %all_to_all.20 = bf16[4,16,5,2048]{3,0,2,1:T(4,128)(2,1)S(1)} all-to-all(bf16[4,16,5,2048]{3,0,2,1:T(4,128)(2,1)S(1)} %copy.61), channel_id=1, replica_groups=mesh['sweep'=2,'expert'=16,'fsdp'=8] {'expert'}, dimensions={1} | all-to-all | bytes 2621440 | tf_op jit(solution)/shard_map/all_to_all | solution.py:50
  172.8 0.7 copy.62
  173.9 67.1 %all_to_all.21 = bf16[8,16,5,2048]{3,1,2,0:T(8,128)(2,1)S(1)} all-to-all(bf16[8,16,5,2048]{3,1,2,0:T(8,128)(2,1)S(1)} %bitcast.70), channel_id=1, replica_groups=mesh['sweep'=2,'expert'=16,'fsdp'=8] {'fsdp'}, dimensions={0} | all-to-all | bytes 5242880 | tf_op jit(solution)/shard_map/all_to_all | solution.py:52
  241.0 3.6 copy.63
  244.5 5.6 %reshape.225 = bf16[640,2048,1]{1,0,2:T(8,128)(2,1)} reshape(bf16[8,16,5,2048]{3,2,1,0:T(8,128)(2,1)} %copy.63) | data formatting | bytes 5242880 | tf_op jit(solution)/shard_map/reshape | solution.py:55
  250.1 7.5 %fusion.6 = f32[2,640,704]{1,2,0:T(8,128)S(1)} fusion(bf16[640,2048,1]{1,0,2:T(8,128)(2,1)} %reshape.225, bf16[1,2,704,2048]{3,2,1,0:T(8,128)(2,1)} %param.14), kind=kOutput, calls=%fused_computation.12 | convolution fusion | flops 3690987520 | bytes 11993088 | tf_op jit(solution)/shard_map/rd,kfd->krf/dot_general | solution.py:10
  257.7 3.8 convolution_convert_fusion
  261.5 5.5 %reshape.194 = bf16[8,16,5,2048]{3,2,1,0:T(8,128)(2,1)} reshape(bf16[640,2048]{1,0:T(8,128)(2,1)} %convolution_convert_fusion) | data formatting | bytes 5242880 | tf_op jit(solution)/shard_map/reshape | solution.py:57
  267.0 4.1 %copy.64 = bf16[8,16,5,2048]{3,1,2,0:T(8,128)(2,1)S(1)} copy(bf16[8,16,5,2048]{3,2,1,0:T(8,128)(2,1)} %reshape.194) | data formatting | bytes 5242880 | tf_op jit(solution)/shard_map/reshape | solution.py:57
  271.0 64.7 %all_to_all.22 = bf16[8,16,5,2048]{3,1,2,0:T(8,128)(2,1)S(1)} all-to-all(bf16[8,16,5,2048]{3,1,2,0:T(8,128)(2,1)S(1)} %copy.64), channel_id=1, replica_groups=mesh['sweep'=2,'expert'=16,'fsdp'=8] {'fsdp'}, dimensions={0} | all-to-all | bytes 5242880 | tf_op jit(solution)/shard_map/all_to_all | solution.py:58
  335.7 0.7 fusion.28
  336.4 4.1 %fusion.10 = bf16[4,16,5,2048]{3,0,2,1:T(4,128)(2,1)} fusion(f32[4,1,16,5,2048]{4,2,3,1,0:T(8,128)S(1)} %get-tuple-element.8, f32[4,1,16,5,2048]{4,2,3,1,0:T(8,128)S(1)} %get-tuple-element.7), kind=kLoop, calls=%fused_computation.15 | loop fusion | flops 1310720 | bytes 6553600 | tf_op jit(solution)/shard_map/convert_element_type | solution.py:60
  340.5 4.9 %all-to-all-start.3 = ((bf16[4,16,5,2048]{3,0,2,1:T(4,128)(2,1)}), bf16[4,16,5,2048]{3,0,2,1:T(4,128)(2,1)S(1)}, u32[]{:S(2)}, u32[]{:S(2)}) async-start(bf16[4,16,5,2048]{3,0,2,1:T(4,128)(2,1)} %fusion.10), calls=%async_computation.3 | async-start | bytes 2621440 | tf_op jit(solution)/shard_map/all_to_all | solution.py:61
  346.0 2.0 gather_fusion.1
  348.3 30.5 %all-to-all-done.3 = bf16[4,16,5,2048]{3,0,2,1:T(4,128)(2,1)S(1)} async-done(((bf16[4,16,5,2048]{3,0,2,1:T(4,128)(2,1)}), bf16[4,16,5,2048]{3,0,2,1:T(4,128)(2,1)S(1)}, u32[]{:S(2)}, u32[]{:S(2)}) %all-to-all-start.3) | async-done | bytes 1310752 | tf_op jit(solution)/shard_map/all_to_all | solution.py:61
  378.8 2.1 copy.67
  380.9 2.6 reshape.195
  383.5 1.4 gather_fusion
  384.8 2.4 reshape.197
  387.2 4.5 %fusion.29 = (f32[128,1,2048]{2,1,0:T(1,128)S(1)}, f32[128,1,2048]{2,1,0:T(1,128)S(1)}) fusion(f32[128,2,2048]{2,1,0:T(2,128)} %reshape.197), kind=kLoop, calls=%fused_computation.58 | loop fusion | bytes 4194304 | tf_op jit(solution)/shard_map/slice | solution.py:63
  391.8 1.9 fusion.13
  (36 shorter events, 2.1 us)
Async XLA Ops:
  6.5 251.1 %copy-start = (bf16[1,704,2048]{2,1,0:T(8,128)(2,1)S(1)}, bf16[1,704,2048]{2,1,0:T(8,128)(2,1)}, u32[]{:S(2)}) copy-start(bf16[1,704,2048]{2,1,0:T(8,128)(2,1)} %param.15) | copy-start | bytes 8650756
  6.6 107.0 %all-gather.2.cloned.1.call-start = ((), (), s32[]{:S(2)}) async-start(), calls=%async_computation.4 | async-start | bytes 8454144 | tf_op jit(solution)/shard_map/all_gather | solution.py:34
  9.6 109.9 %copy-start.6 = (f32[2048]{0:T(1024)S(1)}, f32[2048]{0:T(1024)}, u32[]{:S(2)}) copy-start(f32[2048]{0:T(1024)} %param.11) | copy-start | bytes 24580
  118.5 1.0 copy-start.2
  340.5 4.9 %copy-start.5 = (s32[128,2]{0,1:T(2,128)S(1)}, s32[128,2]{0,1:T(2,128)}, u32[]{:S(2)}) copy-start(s32[128,2]{0,1:T(2,128)} %param.13) | copy-start | bytes 3076
  340.5 5.2 %copy-start.4 = (bf16[2048,64]{0,1:T(8,128)(2,1)S(1)}, bf16[2048,64]{0,1:T(8,128)(2,1)}, u32[]{:S(2)}) copy-start(bf16[2048,64]{0,1:T(8,128)(2,1)} %param.12) | copy-start | bytes 786436
  340.5 38.3 %all-to-all-start.3 = ((bf16[4,16,5,2048]{3,0,2,1:T(4,128)(2,1)}), bf16[4,16,5,2048]{3,0,2,1:T(4,128)(2,1)S(1)}, u32[]{:S(2)}, u32[]{:S(2)}) async-start(bf16[4,16,5,2048]{3,0,2,1:T(4,128)(2,1)} %fusion.10), calls=%async_computation.3 | async-start | bytes 2621440 | tf_op jit(solution)/shard_map/all_to_all | solution.py:61
  387.2 4.6 %copy-start.3 = (f32[128,2048]{1,0:T(8,128)S(1)}, f32[128,2048]{1,0:T(8,128)}, u32[]{:S(2)}) copy-start(f32[128,2048]{1,0:T(8,128)} %copy-done.2) | copy-start | bytes 3145732
  387.2 6.5 %copy-start.1 = (bf16[1,704,2048]{2,1,0:T(8,128)(2,1)S(1)}, bf16[1,704,2048]{2,1,0:T(8,128)(2,1)}, u32[]{:S(2)}) copy-start(bf16[1,704,2048]{2,1,0:T(8,128)(2,1)} %param.15) | copy-start | bytes 8650756
Sparse Core Ops, SparseCore 0:
  10.0 103.5 all-gather.1
where the time goes:
time: 401 us
  blocking collectives  171 us (43%)
  waiting for transfers between devices  135 us (34%)
  local copies, waits for them, and re-layouts  52.4 us (13%)
  matrix products  16.6 us (4%)
  between operations  13.6 us (3%)
  other arithmetic  7.02 us (2%)
  starting transfers between devices  4.88 us (1%)
    all_gather x1, waiting for transfers between devices, on_device(): lax.all_gather(out_proj, ('expert', 'fsdp'), axis=0, tiled=True)  104 us
    all_to_all x1, blocking collectives, on_device(): lax.all_to_all(copies, 'fsdp', split_axis=0, concat_axis=0, tiled=True)  67.1 us
    all_to_all x1, blocking collectives, on_device(): lax.all_to_all(partials, 'fsdp', split_axis=0, concat_axis=0, tiled=True)  64.7 us
    all_to_all x1, blocking collectives, on_device(): lax.all_to_all(outbox, 'expert', split_axis=1, concat_axis=1, tiled=True)  39 us
    all_to_all x1, waiting for transfers between devices, on_device(): lax.all_to_all(summed, 'expert', split_axis=1, concat_axis=1, tiled=True)  30.5 us
    reshape x2, local copies, waits for them, and re-layouts, on_device(): partials = output_half.reshape(members, columns, slots_in, width)  9.54 us
  transfers between devices with their start and end apart: 2, of which 2 were waited for; matrix products, arithmetic and copies ran while one was open for 1% of the time, Pallas kernels for 0%

commit v1 on v0

v1 whole, which is shorter than its diff:
```python
import functools

import jax
import jax.numpy as jnp
from jax import lax
from jax.experimental import pallas as pl
from jax.experimental.pallas import tpu as pltpu
from jax.sharding import PartitionSpec as P


eps_norm = 1e-05
LANES = 128
LIMIT = 10 << 20

VMEM = pltpu.VMEM
SMEM = pltpu.SMEM


def whole(space):
    return pl.BlockSpec(memory_space=space)


def slot_places(expert_ids, experts):
    flat_ids = expert_ids.reshape(-1)
    onehot = (flat_ids[:, None] == jnp.arange(experts, dtype=jnp.int32)[None, :]).astype(jnp.int32)
    before = jnp.cumsum(onehot, axis=0) - onehot
    places = jnp.sum(before * onehot, axis=1)
    return (flat_ids, places)


def project_kernel(offsets, position, context, tokens, *refs):
    blocks, out = refs[:-1], refs[-1]
    count = len(offsets) // 2
    row, core = position[0] // 2, position[0] % 2
    depth = context.shape[1] // len(offsets)
    parts = []
    for away, twin in offsets:
        place = (lax.rem(row + away + count, count) * 2 + (core + twin) % 2) * depth
        parts.append(context[:, pl.ds(pl.multiple_of(place, depth), depth)])
    rows = jnp.concatenate(parts, axis=1)
    step = out.shape[1] // 4

    def piece(n, carry):
        lanes = pl.ds(pl.multiple_of(n * step, step), step)
        total = jnp.dot(
            rows,
            jnp.concatenate([block[:, lanes] for block in blocks], axis=0),
            preferred_element_type=jnp.float32,
        )
        out[:, lanes] = (tokens[:, lanes].astype(jnp.float32) + total).astype(jnp.bfloat16)
        return carry

    lax.fori_loop(0, 4, piece, 0)


def project(offsets, position, context, tokens, blocks):
    return pl.pallas_call(
        functools.partial(project_kernel, offsets),
        in_specs=[whole(SMEM)] + [whole(VMEM)] * (2 + len(blocks)),
        out_specs=whole(VMEM),
        out_shape=jax.ShapeDtypeStruct(tokens.shape, jnp.bfloat16),
        compiler_params=pltpu.CompilerParams(vmem_limit_bytes=LIMIT),
        cost_estimate=pl.CostEstimate(
            flops=2 * tokens.size * context.shape[1], bytes_accessed=2 * tokens.size, transcendentals=0
        ),
    )(position, context, tokens, *blocks)


def front_kernel(index, odd, mine, other, gain, router, ids, box_a, *refs):
    boxes_b, (kept, gates, tiles, box) = refs[:-4], refs[-4:]
    rows, depth = mine.shape
    chunks = 2 * depth // LANES
    half = chunks // 2
    swapped = odd[0] == 1
    own, got = mine[...].astype(jnp.float32), other[...].astype(jnp.float32)
    parts = (jnp.where(swapped, got, own), jnp.where(swapped, own, got))
    squares = sum(jnp.sum(p * p, axis=1, keepdims=True) for p in parts)
    inv_rms = lax.rsqrt(squares / (2 * depth) + eps_norm)
    for c in range(chunks):
        lane = c % half * LANES
        tiles[pl.ds(c, rows, stride=chunks), :] = parts[c // half][:, lane : lane + LANES]
    kept[...] = tiles[...].reshape(rows, chunks, LANES).astype(jnp.bfloat16)
    normed = [
        (p * inv_rms * gain[:, h * depth : (h + 1) * depth]).astype(jnp.bfloat16) for h, p in enumerate(parts)
    ]
    logits = sum(
        jnp.dot(p, router[h * depth : (h + 1) * depth, :], preferred_element_type=jnp.float32)
        for h, p in enumerate(normed)
    )
    lanes = lax.broadcasted_iota(jnp.int32, logits.shape, 1)
    scores = []
    for k in range(2):
        hit = lanes == ids[:, k : k + 1]
        picked = jnp.sum(jnp.where(hit, logits, 0.0), axis=1, keepdims=True)
        scores.append(jax.nn.sigmoid(picked))
    total = scores[0] + scores[1]
    gates[:, 0:1] = scores[0] / total
    gates[:, 1:2] = scores[1] / total
    wider = [p.astype(jnp.float32) for p in normed]
    for c in range(chunks):
        lane = c % half * LANES
        tiles[pl.ds(c, rows, stride=chunks), :] = wider[c // half][:, lane : lane + LANES]
    box[...] = jnp.zeros_like(box)

    def place(t, carry):
        start = pl.multiple_of(t * chunks, chunks)
        line = tiles[pl.ds(start, chunks), :].astype(jnp.bfloat16)
        box[index[2 * t]] = line
        box[index[2 * t + 1]] = line
        return carry

    lax.fori_loop(0, rows, place, 0, unroll=4)
    start = box_a.shape[0]
    box_a[...] = box[:start]
    for part in boxes_b:
        part[...] = box[start : start + part.shape[0]]
        start += part.shape[0]


def front(index, odd, mine, other, gain, router, ids, sizes):
    rows, depth = mine.shape
    chunks = 2 * depth // LANES
    box = lambda n: jax.ShapeDtypeStruct((n, chunks, LANES), jnp.bfloat16)
    got = pl.pallas_call(
        front_kernel,
        in_specs=[whole(SMEM)] * 2 + [whole(VMEM)] * 5,
        out_specs=[whole(VMEM)] * (len(sizes) + 2),
        out_shape=[box(n) for n in sizes] + [box(rows), jax.ShapeDtypeStruct((rows, 2), jnp.float32)],
        scratch_shapes=[VMEM((rows * chunks, LANES), jnp.float32), VMEM((sum(sizes), chunks, LANES), jnp.bfloat16)],
        compiler_params=pltpu.CompilerParams(vmem_limit_bytes=LIMIT),
        cost_estimate=pl.CostEstimate(flops=1 << 24, bytes_accessed=1 << 23, transcendentals=0),
    )(index, odd, mine, other, gain, router, ids)
    return got[0], got[1:-2], got[-2], got[-1]


def dot_t(lhs, rhs):
    return lax.dot_general(lhs, rhs, (((1,), (1,)), ((), ())), preferred_element_type=jnp.float32)


def experts_kernel(count, turns, moves, *refs):
    ins, (gate_up, down), outs = refs[:count], refs[count : count + 2], refs[count + 2 : -4]
    lhs, tiles, both, hidden = refs[-4:]
    rows, wide = lhs.shape
    chunks = wide // LANES
    group = 16
    start = 0
    for block in ins:

        def widen(r, carry, block=block, start=start):
            piece = block[pl.ds(pl.multiple_of(r * group, group), group)].astype(jnp.float32)
            tiles[pl.ds(pl.multiple_of((start + r * group) * chunks, group * chunks), group * chunks), :] = (
                piece.reshape(group * chunks, LANES)
            )
            return carry

        lax.fori_loop(0, block.shape[0] // group, widen, 0)
        start += block.shape[0]

    def spread_lanes(r, carry):
        for c in range(chunks):
            piece = tiles[pl.ds(r * group * chunks + c, group, stride=chunks), :]
            lhs[pl.ds(pl.multiple_of(r * group, group), group), c * LANES : (c + 1) * LANES] = piece.astype(jnp.bfloat16)
        return carry

    lax.fori_loop(0, rows // group, spread_lanes, 0)

    def project_up(k, carry):
        both[k] = dot_t(gate_up[0, k], lhs[...])
        return carry

    lax.fori_loop(0, 2, project_up, 0)
    gate = both[0]
    hidden[...] = (gate / (1.0 + jnp.exp(-gate)) * both[1]).T.astype(jnp.bfloat16)
    step = wide // 4

    def project_down(n, carry):
        part = down[0, :, pl.ds(pl.multiple_of(n * step, step), step)]
        made = jnp.dot(hidden[...], part, preferred_element_type=jnp.float32)
        for c in range(step // LANES):
            tiles[pl.ds(n * (step // LANES) + c, rows, stride=chunks), :] = made[:, c * LANES : (c + 1) * LANES]
        return carry

    lax.fori_loop(0, 4, project_down, 0)

    def settle(turn, carry):
        for out, target, target_step, source, source_step, size in moves:
            place = pl.multiple_of((source + turn * source_step) * chunks, chunks)
            piece = tiles[pl.ds(place, size * chunks), :].reshape(size, chunks, LANES)
            outs[out][pl.ds(target + turn * target_step, size)] = piece.astype(jnp.bfloat16)
        return carry

    lax.fori_loop(0, turns, settle, 0)


def run_experts(ins, w_gate_up, w_down, turns, moves, sizes):
    chunks = ins[0].shape[1]
    rows, wide, units = sum(b.shape[0] for b in ins), chunks * LANES, w_down.shape[1]
    return pl.pallas_call(
        functools.partial(experts_kernel, len(ins), turns, moves),
        in_specs=[whole(VMEM)] * (len(ins) + 2),
        out_specs=[whole(VMEM)] * len(sizes),
        out_shape=[jax.ShapeDtypeStruct((n, chunks, LANES), jnp.bfloat16) for n in sizes],
        scratch_shapes=[
            VMEM((rows, wide), jnp.bfloat16),
            VMEM((rows * chunks, LANES), jnp.float32),
            VMEM((2, units, rows), jnp.float32),
            VMEM((rows, units), jnp.bfloat16),
        ],
        compiler_params=pltpu.CompilerParams(vmem_limit_bytes=2 * LIMIT),
        cost_estimate=pl.CostEstimate(
            flops=6 * rows * wide * units, bytes_accessed=6 * units * wide, transcendentals=rows * units
        ),
    )(*ins, w_gate_up, w_down)


def back_kernel(index, gates, *refs):
    boxes, (kept, out, tiles, box) = refs[:-4], refs[-4:]
    rows, chunks, _ = kept.shape
    start = 0
    for part in boxes:
        box[start : start + part.shape[0]] = part[...]
        start += part.shape[0]

    def token(t, carry):
        value = kept[t].astype(jnp.float32)
        for k in range(2):
            value = value + gates[2 * t + k] * box[index[2 * t + k]].astype(jnp.float32)
        tiles[pl.ds(pl.multiple_of(t * chunks, chunks), chunks), :] = value
        return carry

    lax.fori_loop(0, rows, token, 0, unroll=4)
    for c in range(chunks):
        out[:, c * LANES : (c + 1) * LANES] = tiles[pl.ds(c, rows, stride=chunks), :].astype(jnp.bfloat16)


def back(index, gates, boxes, kept):
    rows, chunks, _ = kept.shape
    total = sum(b.shape[0] for b in boxes)
    return pl.pallas_call(
        back_kernel,
        in_specs=[whole(SMEM)] * 2 + [whole(VMEM)] * (len(boxes) + 1),
        out_specs=whole(VMEM),
        out_shape=jax.ShapeDtypeStruct((rows, chunks * LANES), jnp.bfloat16),
        scratch_shapes=[VMEM((rows * chunks, LANES), jnp.float32), VMEM((total, chunks, LANES), jnp.bfloat16)],
        compiler_params=pltpu.CompilerParams(vmem_limit_bytes=LIMIT),
        cost_estimate=pl.CostEstimate(flops=1 << 20, bytes_accessed=1 << 22, transcendentals=0),
    )(index, gates, *boxes, kept)


def on_device(tokens, context, out_proj, norm_gain, router, expert_ids, w_gate_up, w_down):
    rows_here, width = tokens.shape
    columns = lax.axis_size("expert")
    members = lax.axis_size("fsdp")
    experts = columns * members // 2
    group = members // 2
    slot_cap = 5 * rows_here // (2 * experts)
    chunks = width // LANES
    assert group == 4

    def shift(even, odd):
        return [(i, (i + (odd if i % 2 else even)) % members) for i in range(members)]

    out_hops = (shift(-1, 1), shift(2, -2), shift(-3, 3))
    back_hops = tuple([(b, a) for a, b in hop] for hop in out_hops)
    swap = [(i, i ^ 1) for i in range(members)]

    def swapped(value):
        return lax.ppermute(value, "fsdp", swap)

    def spread(blocks, hops):
        return [blocks[0]] + [lax.ppermute(b, "fsdp", hop) for b, hop in zip(blocks[1:], hops)]

    def across(box):
        boxes = box.reshape(columns, -1, chunks, LANES)
        return lax.all_to_all(boxes, "expert", split_axis=0, concat_axis=0, tiled=True).reshape(box.shape)

    def split(box):
        parts = box.reshape(columns, group, -1, chunks, LANES)
        return [parts[:, m].reshape(-1, chunks, LANES) for m in range(group)]

    def join(blocks):
        parts = [b.reshape(columns, 1, -1, chunks, LANES) for b in blocks]
        return jnp.concatenate(parts, axis=1).reshape(-1, chunks, LANES)

    def add_halves(own, other):
        return (own.astype(jnp.float32) + other.astype(jnp.float32)).astype(jnp.bfloat16)

    here = lax.axis_index("fsdp")
    odd = here % 2
    depth = width // 2
    tokens_of = lambda h: lax.dynamic_slice_in_dim(tokens, h * depth, depth, axis=1)
    their_context = swapped(context)
    their_tokens = swapped(tokens_of(1 - odd))
    pieces = jnp.stack([out_proj[:, :depth], out_proj[:, depth:]])
    pieces = jnp.broadcast_to(pieces[None], (group,) + pieces.shape).reshape(members, -1, depth)
    pieces = lax.all_to_all(pieces, "fsdp", split_axis=0, concat_axis=0, tiled=True)
    block = pieces.reshape(-1, depth)
    hop = lambda value, by: lax.ppermute(value, "expert", [(i, (i + by) % columns) for i in range(columns)])
    twin = lambda value: lax.ppermute(value, "expert", [(i, i ^ 1) for i in range(columns)])
    upward, downward, held, offsets = [block], [block], [block], [(0, 0)]
    reach = columns // 4
    for k in range(1, reach):
        upward.append(hop(upward[-1], 2))
        downward.append(hop(downward[-1], -2))
        held.append(jnp.concatenate([upward[k], downward[k]], axis=0))
        offsets += [(-k, 0), (k, 0)]
    cut = block.shape[0] // 2
    ends = [hop(upward[-1][:cut], 2), hop(downward[-1][cut:], -2)]
    held.append(jnp.concatenate(ends, axis=0))
    offsets.append((reach, 0))
    held += [twin(v) for v in held]
    offsets = tuple(offsets + [(away, 1) for away, _ in offsets])
    position = lax.axis_index("expert").astype(jnp.int32).reshape(1)

    flat_ids, places = slot_places(expert_ids, experts)
    away = (flat_ids % group - here // 2) % group
    message = jnp.where(away == 0, 0, jnp.where(away == 2, 3, jnp.where((away == 1) == (odd == 0), 2, 1)))
    column = flat_ids // group
    cap_b = slot_cap // 2
    cap_a = slot_cap - cap_b
    lines = columns * group
    by_column = column * group + message
    by_message = message * columns + column
    early = places < cap_a
    first = lines * cap_a
    index_out = jnp.where(early, by_column * cap_a + places, first + by_message * cap_b + places - cap_a)
    index_in = jnp.where(early, by_message * cap_a + places, first + by_column * cap_b + places - cap_a)
    index_out, index_in = index_out.astype(jnp.int32), index_in.astype(jnp.int32)
    moves_a = tuple(
        (d, m * cap_a, group * cap_a, (d * group + m) * columns * cap_a, cap_a, cap_a)
        for d in range(2)
        for m in range(group)
    )
    moves_b = tuple(
        (2 * d + (m > 0), max(m - 1, 0) * columns * cap_b, cap_b, (d * lines + m) * cap_b, group * cap_b, cap_b)
        for d in range(2)
        for m in range(group)
    )

    other = swapped(project(offsets, position, their_context, their_tokens, held))
    mine = project(offsets, position, context, tokens_of(odd), held)
    sizes = [lines * cap_a] + [columns * cap_b] * group
    box_a, boxes_b, kept, gates = front(
        index_out,
        odd.astype(jnp.int32).reshape(1),
        mine,
        other,
        norm_gain.reshape(1, width),
        router,
        expert_ids,
        sizes,
    )

    over_a = across(box_a)
    near_b = spread(boxes_b, out_hops)
    near_b = across(join(near_b))
    near_a = spread(split(over_a), out_hops)
    far_a = [swapped(b) for b in near_a]
    far_b = swapped(near_b)

    own_a, other_a = run_experts(near_a + far_a, w_gate_up, w_down, columns, moves_a, [lines * cap_a] * 2)
    sum_a = add_halves(own_a, swapped(other_a))
    few = columns * cap_b
    made_b = run_experts([near_b, far_b], w_gate_up, w_down, columns, moves_b, [few, (group - 1) * few] * 2)
    going = add_halves(made_b[1], swapped(made_b[3]))
    staying = add_halves(made_b[0], swapped(made_b[2]))
    sum_b = [staying] + [going[m * few : (m + 1) * few] for m in range(group - 1)]
    sum_a = across(sum_a)
    sum_b = join(spread(sum_b, back_hops))
    done_b = across(sum_b)
    done_a = spread(split(sum_a), back_hops)
    return back(index_in, gates.reshape(-1), done_a + [done_b], kept)


def solution(mesh):
    rows = P(("sweep", "expert", "fsdp"), None)
    return jax.shard_map(
        on_device,
        mesh=mesh,
        in_specs=(
            rows,
            rows,
            rows,
            P("sweep"),
            P("sweep", None),
            rows,
            P(("sweep", "expert", "fsdp"), None, None, None),
            P(("sweep", "expert", "fsdp"), None, None),
        ),
        out_specs=rows,
        check_vma=False,
    )
```

time: 401 us -> 263 us (0.66)
  blocking collectives: 171 us -> 17 us
  starting transfers between devices: 4.88 us -> 95.7 us
  waiting for transfers between devices: 135 us -> 98.6 us
  local copies, waits for them, and re-layouts: 52.4 us -> 16.1 us
  Pallas kernels: 0 us -> 27.8 us
  matrix products: 16.6 us -> 0 us
  between operations: 13.6 us -> 0.35 us
    all_to_all x3 -> x1, blocking collectives: 171 us -> 17 us  [on_device(): lax.all_to_all(pieces, 'fsdp', split_axis=0, concat_axis=0, tiled=True)]
    all_gather x1 -> x0, waiting for transfers between devices: 104 us -> none  [on_device(): lax.all_gather(out_proj, ('expert', 'fsdp'), axis=0, tiled=True)]
    ppermute x0 -> x36, starting transfers between devices: none -> 66.8 us  [the longest x8 21.1 us: on_device(): lax.ppermute(value, 'expert', [(i, (i + by) % columns) for i in range(col...]
    ppermute x0 -> x36, waiting for transfers between devices: none -> 65.1 us  [the longest x11 33.5 us: swapped(): return lax.ppermute(value, 'fsdp', swap)]
    pallas_call x0 -> x6, Pallas kernels: none -> 27.8 us  [the longest x2 16.4 us: run_experts(): pl.pallas_call(functools.partial(experts_kernel, len(ins), turns, moves),...]
    reshape x8 -> x1, local copies, waits for them, and re-layouts: 26.3 us -> 0.13 us  [on_device(): return back(index_in, gates.reshape(-1), done_a + [done_b], kept)]
    all_to_all x1 -> x4, starting transfers between devices: 4.88 us -> 28.9 us  [across(): lax.all_to_all(boxes, 'expert', split_axis=0, concat_axis=0, tiled=True)]
    dot_general x4 -> x0, matrix products: 16.6 us -> none  [the longest x1 7.51 us: half_block(): jnp.einsum('rd,kfd->krf', taken, gate_up_w, preferred_element_type=jnp.fl...]
  transfers between devices with their start and end apart: 2 -> 40, of which waited for: 2 -> 16; matrix products, arithmetic and copies ran while one was open for 1% -> 5% of each run, Pallas kernels for 0% -> 7%
where the time goes in v1:
time: 263 us; the launch traced here: 260 us
  waiting for transfers between devices  98.6 us (37%)
  starting transfers between devices  95.7 us (36%)
  Pallas kernels  27.8 us (11%)
  blocking collectives  17 us (6%)
  local copies, waits for them, and re-layouts  16.1 us (6%)
  other arithmetic  4.66 us (2%)
    all_to_all x4, waiting for transfers between devices, across(): lax.all_to_all(boxes, 'expert', split_axis=0, concat_axis=0, tiled=True)  33.6 us
    ppermute x11, waiting for transfers between devices, swapped(): return lax.ppermute(value, 'fsdp', swap)  33.5 us
    all_to_all x4, starting transfers between devices, across(): lax.all_to_all(boxes, 'expert', split_axis=0, concat_axis=0, tiled=True)  28.9 us
    ppermute x12, waiting for transfers between devices, spread(): lax.ppermute(b, 'fsdp', hop)  22.6 us
    ppermute x8, starting transfers between devices, on_device(): lax.ppermute(value, 'expert', [(i, (i + by) % columns) for i in range(col...  21.1 us
    ppermute x12, starting transfers between devices, spread(): lax.ppermute(b, 'fsdp', hop)  17.9 us
    all_to_all x1, blocking collectives, on_device(): lax.all_to_all(pieces, 'fsdp', split_axis=0, concat_axis=0, tiled=True)  17 us
    ppermute x5, starting transfers between devices, on_device(): lax.ppermute(value, 'expert', [(i, i ^ 1) for i in range(columns)])  16.7 us
  transfers between devices with their start and end apart: 40, of which 16 were waited for; matrix products, arithmetic and copies ran while one was open for 5% of the time, Pallas kernels for 7%

profile of v1, /device:TPU:513, one launch (start us, length us, event | category | flops | bytes accessed | tf_op | source)
XLA Modules:
  0.0 260.3 jit_solution(9414189446542378698)
XLA Ops:
  0.9 17.0 %all_to_all.25 = bf16[8,16,1024]{2,1,0:T(8,128)(2,1)S(1)} all-to-all(bf16[8,16,1024]{2,1,0:T(8,128)(2,1)S(1)} %bitcast.66), channel_id=1, replica_groups=mesh['sweep'=2,'expert'=16,'fsdp'=8] {'fsdp'}, dimensions={0} | all-to-all | bytes 524288 | tf_op jit(solution)/shard_map/all_to_all | solution.py:296
  17.9 3.8 %collective-permute-start = (bf16[128,1024]{1,0:T(8,128)(2,1)S(1)}, bf16[128,1024]{1,0:T(8,128)(2,1)S(1)}, u32[]{:S(2)}, u32[]{:S(2)}) collective-permute-start(bf16[128,1024]{1,0:T(8,128)(2,1)S(1)} %bitcast.52), channel_id=1, source_target_pairs={{0,16},{8,24},{16,32},{24,40},{32,48},{40,56},{48,64},{56,72},{64,... | collective-permute-start | bytes 786440 | tf_op jit(solution)/shard_map/ppermute | solution.py:298
  21.6 9.1 %collective-permute-start.1 = (bf16[128,1024]{1,0:T(8,128)(2,1)S(1)}, bf16[128,1024]{1,0:T(8,128)(2,1)S(1)}, u32[]{:S(2)}, u32[]{:S(2)}) collective-permute-start(bf16[128,1024]{1,0:T(8,128)(2,1)S(1)} %bitcast.53), channel_id=1, source_target_pairs={{0,112},{8,120},{16,0},{24,8},{32,16},{40,24},{48,32},{56,40},{64,... | collective-permute-start | bytes 786440 | tf_op jit(solution)/shard_map/ppermute | solution.py:298
  30.7 3.8 %collective-permute-done = bf16[128,1024]{1,0:T(8,128)(2,1)S(1)} collective-permute-done((bf16[128,1024]{1,0:T(8,128)(2,1)S(1)}, bf16[128,1024]{1,0:T(8,128)(2,1)S(1)}, u32[]{:S(2)}, u32[]{:S(2)}) %collective-permute-start) | collective-permute-done | bytes 262176 | tf_op jit(solution)/shard_map/ppermute | solution.py:298
  34.5 2.7 %collective-permute-start.3 = (bf16[128,1024]{1,0:T(8,128)(2,1)S(1)}, bf16[128,1024]{1,0:T(8,128)(2,1)S(1)}, u32[]{:S(2)}, u32[]{:S(2)}) collective-permute-start(bf16[128,1024]{1,0:T(8,128)(2,1)S(1)} %collective-permute-done.1), channel_id=1, source_target_pairs={{0,112},{8,120},{16,0},{24,8},{32,16},{40,24},{48,32},{56,40},{64,... | collective-permute-start | bytes 786440 | tf_op jit(solution)/shard_map/ppermute | solution.py:298
  40.8 3.1 %collective-permute-done.2 = bf16[128,1024]{1,0:T(8,128)(2,1)S(1)} collective-permute-done((bf16[128,1024]{1,0:T(8,128)(2,1)S(1)}, bf16[128,1024]{1,0:T(8,128)(2,1)S(1)}, u32[]{:S(2)}, u32[]{:S(2)}) %collective-permute-start.2) | collective-permute-done | bytes 262176 | tf_op jit(solution)/shard_map/ppermute | solution.py:298
  43.9 2.7 %collective-permute-start.5 = (bf16[128,1024]{1,0:T(8,128)(2,1)S(1)}, bf16[128,1024]{1,0:T(8,128)(2,1)S(1)}, u32[]{:S(2)}, u32[]{:S(2)}) collective-permute-start(bf16[128,1024]{1,0:T(8,128)(2,1)S(1)} %collective-permute-done.3), channel_id=1, source_target_pairs={{0,112},{8,120},{16,0},{24,8},{32,16},{40,24},{48,32},{56,40},{64,... | collective-permute-start | bytes 786440 | tf_op jit(solution)/shard_map/ppermute | solution.py:298
  46.5 10.6 %collective-permute-start.9 = (bf16[256,1024]{1,0:T(8,128)(2,1)S(1)}, bf16[256,1024]{1,0:T(8,128)(2,1)S(1)}, u32[]{:S(2)}, u32[]{:S(2)}) collective-permute-start(bf16[256,1024]{1,0:T(8,128)(2,1)S(1)} %constant_dynamic-update-slice_fusion.refs_1_), channel_id=1, source_target_pairs={{0,8},{8,0},{16,24},{24,16},{32,40},{40,32},{48,56},{56,48},{64,72... | collective-permute-start | bytes 1572872 | tf_op jit(solution)/shard_map/ppermute | solution.py:299
  57.4 2.8 %collective-permute-start.7 = (bf16[64,1024]{1,0:T(8,128)(2,1)S(1)}, bf16[64,1024]{1,0:T(8,128)(2,1)S(1)}, u32[]{:S(2)}, u32[]{:S(2)}) collective-permute-start(bf16[64,1024]{1,0:T(8,128)(2,1)S(1)} %slice.70), channel_id=1, source_target_pairs={{0,112},{8,120},{16,0},{24,8},{32,16},{40,24},{48,32},{56,40},{64,... | collective-permute-start | bytes 393224 | tf_op jit(solution)/shard_map/ppermute | solution.py:298
  62.4 5.3 %collective-permute-start.10 = (bf16[256,1024]{1,0:T(8,128)(2,1)S(1)}, bf16[256,1024]{1,0:T(8,128)(2,1)S(1)}, u32[]{:S(2)}, u32[]{:S(2)}) collective-permute-start(bf16[256,1024]{1,0:T(8,128)(2,1)S(1)} %constant_dynamic-update-slice_fusion.2.refs_2_), channel_id=1, source_target_pairs={{0,8},{8,0},{16,24},{24,16},{32,40},{40,32},{48,56},{56,48},{64,72... | collective-permute-start | bytes 1572872 | tf_op jit(solution)/shard_map/ppermute | solution.py:299
  72.3 3.1 %shard_map.83 = bf16[128,1024]{1,0:T(8,128)(2,1)S(1)} custom-call(s32[1]{0:T(128)} %bitcast.2.position, bf16[128,2048]{1,0:T(8,128)(2,1)} %collective-permute-done.13.context, bf16[128,1024]{1,0:T(8,128)(2,1)} %collective-permute-done.14.tokens, bf16[128,1024]{1,0:T(8,128)(2,1)S(1)} %bitcast.55, ...), custom_call_target="tpu_custom_call" | custom-call | flops 536870912 | bytes 262144 | tf_op jit(solution)/shard_map/pallas_call | solution.py:57
  75.5 2.8 %shard_map.82.mine = bf16[128,1024]{1,0:T(8,128)(2,1)S(1)} custom-call(s32[1]{0:T(128)} %bitcast.2.position, bf16[128,2048]{1,0:T(8,128)(2,1)S(1)} %copy-done.8, bf16[128,1024]{1,0:T(8,128)(2,1)S(1)} %copy-done.3, bf16[128,1024]{1,0:T(8,128)(2,1)S(1)} %bitcast.56, bf16[256,1024]{1,0:T(8,128)(2,1)S(1)} %constant_dynamic-update-slice_fusion.refs_1_, ...), custom_call_target="tpu_custom_call" | custom-call | flops 536870912 | bytes 262144 | tf_op jit(solution)/shard_map/pallas_call | solution.py:57
  78.3 4.8 %collective-permute-done.15.other = bf16[128,1024]{1,0:T(8,128)(2,1)S(1)} collective-permute-done((bf16[128,1024]{1,0:T(8,128)(2,1)S(1)}, bf16[128,1024]{1,0:T(8,128)(2,1)S(1)}, u32[]{:S(2)}, u32[]{:S(2)}) %collective-permute-start.15) | collective-permute-done | bytes 262176 | tf_op jit(solution)/shard_map/ppermute | solution.py:268
  83.1 3.2 %shard_map.84 = (bf16[192,16,128]{2,1,0:T(8,128)(2,1)}, bf16[32,16,128]{2,1,0:T(8,128)(2,1)S(1)}, bf16[32,16,128]{2,1,0:T(8,128)(2,1)S(1)}, bf16[32,16,128]{2,1,...) custom-call(s32[256]{0:T(256)S(1)} %get-tuple-element.31.index, ...), custom_call_target="tpu_custom_call" | custom-call | flops 16777216 | bytes 8388608 | tf_op jit(solution)/shard_map/pallas_call | solution.py:124
  86.3 4.7 %all-to-all-start.1 = ((bf16[16,12,16,128]{3,2,1,0:T(8,128)(2,1)}), bf16[16,12,16,128]{3,2,1,0:T(8,128)(2,1)S(1)}, u32[]{:S(2)}, u32[]{:S(2)}) async-start(bf16[16,12,16,128]{3,2,1,0:T(8,128)(2,1)} %bitcast.8), calls=%async_computation.1 | async-start | bytes 1572864 | tf_op jit(solution)/shard_map/all_to_all | solution.py:275
  91.1 22.7 %all-to-all-done.1 = bf16[16,12,16,128]{3,2,1,0:T(8,128)(2,1)S(1)} async-done(((bf16[16,12,16,128]{3,2,1,0:T(8,128)(2,1)}), bf16[16,12,16,128]{3,2,1,0:T(8,128)(2,1)S(1)}, u32[]{:S(2)}, u32[]{:S(2)}) %all-to-all-start.1) | async-done | bytes 786464 | tf_op jit(solution)/shard_map/all_to_all | solution.py:275
  119.4 3.4 %collective-permute-start.29 = (bf16[32,16,128]{2,1,0:T(8,128)(2,1)S(1)}, bf16[32,16,128]{2,1,0:T(8,128)(2,1)S(1)}, u32[]{:S(2)}, u32[]{:S(2)}) collective-permute-start(bf16[32,16,128]{2,1,0:T(8,128)(2,1)S(1)} %get-tuple-element.25), channel_id=1, source_target_pairs={{0,5},{1,4},{2,7},{3,6},{4,1},{5,0},{6,3},{7,2},{8,13},{9,12},{10,... | collective-permute-start | bytes 393224 | tf_op jit(solution)/shard_map/ppermute | solution.py:271
  122.8 2.8 %collective-permute-done.28 = bf16[32,16,128]{2,1,0:T(8,128)(2,1)S(1)} collective-permute-done((bf16[32,16,128]{2,1,0:T(8,128)(2,1)S(1)}, bf16[32,16,128]{2,1,0:T(8,128)(2,1)S(1)}, u32[]{:S(2)}, u32[]{:S(2)}) %collective-permute-start.28) | collective-permute-done | bytes 131104 | tf_op jit(solution)/shard_map/ppermute | solution.py:271
  125.6 10.5 %collective-permute-done.16.refs_1_ = bf16[48,16,128]{2,1,0:T(8,128)(2,1)} collective-permute-done((bf16[48,16,128]{2,1,0:T(8,128)(2,1)S(1)}, bf16[48,16,128]{2,1,0:T(8,128)(2,1)}, u32[]{:S(2)}, u32[]{:S(2)}) %collective-permute-start.16) | collective-permute-done | bytes 196640 | tf_op jit(solution)/shard_map/ppermute | solution.py:271
  137.6 3.7 %collective-permute-start.22 = (bf16[48,16,128]{2,1,0:T(8,128)(2,1)}, bf16[48,16,128]{2,1,0:T(8,128)(2,1)}, u32[]{:S(2)}, u32[]{:S(2)}) collective-permute-start(bf16[48,16,128]{2,1,0:T(8,128)(2,1)} %collective-permute-done.18.refs_3_), channel_id=1, source_target_pairs={{0,1},{1,0},{2,3},{3,2},{4,5},{5,4},{6,7},{7,6},{8,9},{9,8},{10,11... | collective-permute-start | bytes 589832 | tf_op jit(solution)/shard_map/ppermute | solution.py:268
  143.4 4.6 %all-to-all-start.3 = ((bf16[16,8,16,128]{3,2,1,0:T(8,128)(2,1)}), bf16[16,8,16,128]{3,2,1,0:T(8,128)(2,1)S(1)}, u32[]{:S(2)}, u32[]{:S(2)}) async-start(bf16[16,8,16,128]{3,2,1,0:T(8,128)(2,1)} %bitcast.65), calls=%async_computation.3 | async-start | bytes 1048576 | tf_op jit(solution)/shard_map/all_to_all | solution.py:275
  148.2 2.6 collective-permute-done.22.refs_7_
  150.7 2.6 %copy-done = bf16[1,2,704,2048]{3,2,1,0:T(8,128)(2,1)S(1)} copy-done((bf16[1,2,704,2048]{3,2,1,0:T(8,128)(2,1)S(1)}, bf16[1,2,704,2048]{3,2,1,0:T(8,128)(2,1)}, u32[]{:S(2)}) %copy-start) | copy-done | bytes 5767192
  153.4 10.2 %shard_map.85 = (bf16[192,16,128]{2,1,0:T(8,128)(2,1)S(1)}, bf16[192,16,128]{2,1,0:T(8,128)(2,1)}) custom-call(bf16[48,16,128]{2,1,0:T(8,128)(2,1)} %bitcast.10.refs_0_, bf16[48,16,128]{2,1,0:T(8,128)(2,1)} %collective-permute-done.16.refs_1_, bf16[48,16,128]{2,1,0:T(8,128)(2,1)} %collective-permute-done.17.refs_2_, ...), custom_call_target="tpu_custom_call" | custom-call | flops 3321888768 | bytes 8650752 | tf_op jit(solution)/shard_map/pallas_call | solution.py:198
  166.7 17.2 %collective-permute-done.23 = bf16[192,16,128]{2,1,0:T(8,128)(2,1)} collective-permute-done((bf16[192,16,128]{2,1,0:T(8,128)(2,1)}, bf16[192,16,128]{2,1,0:T(8,128)(2,1)}, u32[]{:S(2)}, u32[]{:S(2)}) %collective-permute-start.23) | collective-permute-done | bytes 786464 | tf_op jit(solution)/shard_map/ppermute | solution.py:268
  186.4 8.7 %all-to-all-start.2 = ((bf16[16,12,16,128]{3,2,1,0:T(8,128)(2,1)}), bf16[16,12,16,128]{3,2,1,0:T(8,128)(2,1)}, u32[]{:S(2)}, u32[]{:S(2)}) async-start(bf16[16,12,16,128]{3,2,1,0:T(8,128)(2,1)} %bitcast.64), calls=%async_computation.2 | async-start | bytes 1572864 | tf_op jit(solution)/shard_map/all_to_all | solution.py:275
  195.2 2.6 %copy-done.1 = bf16[1,2,704,2048]{3,2,1,0:T(8,128)(2,1)S(1)} copy-done((bf16[1,2,704,2048]{3,2,1,0:T(8,128)(2,1)S(1)}, bf16[1,2,704,2048]{3,2,1,0:T(8,128)(2,1)}, u32[]{:S(2)}) %copy-start.1) | copy-done | bytes 5767192
  197.8 6.2 %shard_map.86 = (bf16[32,16,128]{2,1,0:T(8,128)(2,1)S(1)}, bf16[96,16,128]{2,1,0:T(8,128)(2,1)S(1)}, bf16[32,16,128]{2,1,0:T(8,128)(2,1)S(1)}, bf16[96,16,128]{2,1,0:T(8,128)(2,1)S(1)}) custom-call(bf16[128,16,128]{2,1,0:T(8,128)(2,1)S(1)} %bitcast.58, bf16[128,16,128]{2,1,0:T(8,128)(2,1)} %collective-permute-done.30.refs_1_, ...), custom_call_target="tpu_custom_call" | custom-call | flops 2214592512 | bytes 8650752 | tf_op jit(solution)/shard_map/pallas_call | solution.py:198
  206.0 8.7 %collective-permute-done.32 = bf16[96,16,128]{2,1,0:T(8,128)(2,1)S(1)} collective-permute-done((bf16[96,16,128]{2,1,0:T(8,128)(2,1)S(1)}, bf16[96,16,128]{2,1,0:T(8,128)(2,1)S(1)}, u32[]{:S(2)}, u32[]{:S(2)}) %collective-permute-start.32) | collective-permute-done | bytes 393248 | tf_op jit(solution)/shard_map/ppermute | solution.py:268
  222.3 4.4 %collective-permute-done.35 = bf16[32,16,128]{2,1,0:T(8,128)(2,1)S(1)} collective-permute-done((bf16[32,16,128]{2,1,0:T(8,128)(2,1)S(1)}, bf16[32,16,128]{2,1,0:T(8,128)(2,1)S(1)}, u32[]{:S(2)}, u32[]{:S(2)}) %collective-permute-start.35) | collective-permute-done | bytes 131104 | tf_op jit(solution)/shard_map/ppermute | solution.py:271
  227.6 10.8 %all-to-all-start.4 = ((bf16[16,8,16,128]{3,2,1,0:T(8,128)(2,1)}), bf16[16,8,16,128]{3,2,1,0:T(8,128)(2,1)S(1)}, u32[]{:S(2)}, u32[]{:S(2)}) async-start(bf16[16,8,16,128]{3,2,1,0:T(8,128)(2,1)} %bitcast.30), calls=%async_computation.4 | async-start | bytes 1048576 | tf_op jit(solution)/shard_map/all_to_all | solution.py:275
  244.8 10.9 %all-to-all-done.4 = bf16[16,8,16,128]{3,2,1,0:T(8,128)(2,1)S(1)} async-done(((bf16[16,8,16,128]{3,2,1,0:T(8,128)(2,1)}), bf16[16,8,16,128]{3,2,1,0:T(8,128)(2,1)S(1)}, u32[]{:S(2)}, u32[]{:S(2)}) %all-to-all-start.4) | async-done | bytes 524320 | tf_op jit(solution)/shard_map/all_to_all | solution.py:275
  (118 shorter events, 48.0 us)
Async XLA Ops:
  17.9 16.6 %collective-permute-start = (bf16[128,1024]{1,0:T(8,128)(2,1)S(1)}, bf16[128,1024]{1,0:T(8,128)(2,1)S(1)}, u32[]{:S(2)}, u32[]{:S(2)}) collective-permute-start(bf16[128,1024]{1,0:T(8,128)(2,1)S(1)} %bitcast.52), channel_id=1, source_target_pairs={{0,16},{8,24},{16,32},{24,40},{32,48},{40,56},{48,64},{56,72},{64,... | collective-permute-start | bytes 786440 | tf_op jit(solution)/shard_map/ppermute | solution.py:298
  21.6 12.9 %collective-permute-start.1 = (bf16[128,1024]{1,0:T(8,128)(2,1)S(1)}, bf16[128,1024]{1,0:T(8,128)(2,1)S(1)}, u32[]{:S(2)}, u32[]{:S(2)}) collective-permute-start(bf16[128,1024]{1,0:T(8,128)(2,1)S(1)} %bitcast.53), channel_id=1, source_target_pairs={{0,112},{8,120},{16,0},{24,8},{32,16},{40,24},{48,32},{56,40},{64,... | collective-permute-start | bytes 786440 | tf_op jit(solution)/shard_map/ppermute | solution.py:298
  34.5 9.4 %collective-permute-start.2 = (bf16[128,1024]{1,0:T(8,128)(2,1)S(1)}, bf16[128,1024]{1,0:T(8,128)(2,1)S(1)}, u32[]{:S(2)}, u32[]{:S(2)}) collective-permute-start(bf16[128,1024]{1,0:T(8,128)(2,1)S(1)} %collective-permute-done), channel_id=1, source_target_pairs={{0,16},{8,24},{16,32},{24,40},{32,48},{40,56},{48,64},{56,72},{64,... | collective-permute-start | bytes 786440 | tf_op jit(solution)/shard_map/ppermute | solution.py:298
  34.5 9.4 %collective-permute-start.3 = (bf16[128,1024]{1,0:T(8,128)(2,1)S(1)}, bf16[128,1024]{1,0:T(8,128)(2,1)S(1)}, u32[]{:S(2)}, u32[]{:S(2)}) collective-permute-start(bf16[128,1024]{1,0:T(8,128)(2,1)S(1)} %collective-permute-done.1), channel_id=1, source_target_pairs={{0,112},{8,120},{16,0},{24,8},{32,16},{40,24},{48,32},{56,40},{64,... | collective-permute-start | bytes 786440 | tf_op jit(solution)/shard_map/ppermute | solution.py:298
  39.0 30.0 %collective-permute-start.14 = (bf16[128,1024]{1,0:T(8,128)(2,1)}, bf16[128,1024]{1,0:T(8,128)(2,1)}, u32[]{:S(2)}, u32[]{:S(2)}) collective-permute-start(bf16[128,1024]{1,0:T(8,128)(2,1)} %get-tuple-element.42), channel_id=1, source_target_pairs={{0,1},{1,0},{2,3},{3,2},{4,5},{5,4},{6,7},{7,6},{8,9},{9,8},{10,11... | collective-permute-start | bytes 786440 | tf_op jit(solution)/shard_map/ppermute | solution.py:268
  39.0 30.5 %collective-permute-start.13 = (bf16[128,2048]{1,0:T(8,128)(2,1)S(1)}, bf16[128,2048]{1,0:T(8,128)(2,1)}, u32[]{:S(2)}, u32[]{:S(2)}) collective-permute-start(bf16[128,2048]{1,0:T(8,128)(2,1)S(1)} %copy-done.7), channel_id=1, source_target_pairs={{0,1},{1,0},{2,3},{3,2},{4,5},{5,4},{6,7},{7,6},{8,9},{9,8},{10,11... | collective-permute-start | bytes 1572872 | tf_op jit(solution)/shard_map/ppermute | solution.py:268
  43.8 13.4 %collective-permute-start.4 = (bf16[128,1024]{1,0:T(8,128)(2,1)S(1)}, bf16[128,1024]{1,0:T(8,128)(2,1)S(1)}, u32[]{:S(2)}, u32[]{:S(2)}) collective-permute-start(bf16[128,1024]{1,0:T(8,128)(2,1)S(1)} %collective-permute-done.2), channel_id=1, source_target_pairs={{0,16},{8,24},{16,32},{24,40},{32,48},{40,56},{48,64},{56,72},{64,... | collective-permute-start | bytes 786440 | tf_op jit(solution)/shard_map/ppermute | solution.py:298
  43.9 13.5 %collective-permute-start.5 = (bf16[128,1024]{1,0:T(8,128)(2,1)S(1)}, bf16[128,1024]{1,0:T(8,128)(2,1)S(1)}, u32[]{:S(2)}, u32[]{:S(2)}) collective-permute-start(bf16[128,1024]{1,0:T(8,128)(2,1)S(1)} %collective-permute-done.3), channel_id=1, source_target_pairs={{0,112},{8,120},{16,0},{24,8},{32,16},{40,24},{48,32},{56,40},{64,... | collective-permute-start | bytes 786440 | tf_op jit(solution)/shard_map/ppermute | solution.py:298
  46.5 25.7 %collective-permute-start.9 = (bf16[256,1024]{1,0:T(8,128)(2,1)S(1)}, bf16[256,1024]{1,0:T(8,128)(2,1)S(1)}, u32[]{:S(2)}, u32[]{:S(2)}) collective-permute-start(bf16[256,1024]{1,0:T(8,128)(2,1)S(1)} %constant_dynamic-update-slice_fusion.refs_1_), channel_id=1, source_target_pairs={{0,8},{8,0},{16,24},{24,16},{32,40},{40,32},{48,56},{56,48},{64,72... | collective-permute-start | bytes 1572872 | tf_op jit(solution)/shard_map/ppermute | solution.py:299
  57.4 10.9 %collective-permute-start.7 = (bf16[64,1024]{1,0:T(8,128)(2,1)S(1)}, bf16[64,1024]{1,0:T(8,128)(2,1)S(1)}, u32[]{:S(2)}, u32[]{:S(2)}) collective-permute-start(bf16[64,1024]{1,0:T(8,128)(2,1)S(1)} %slice.70), channel_id=1, source_target_pairs={{0,112},{8,120},{16,0},{24,8},{32,16},{40,24},{48,32},{56,40},{64,... | collective-permute-start | bytes 393224 | tf_op jit(solution)/shard_map/ppermute | solution.py:298
  62.4 9.8 %collective-permute-start.10 = (bf16[256,1024]{1,0:T(8,128)(2,1)S(1)}, bf16[256,1024]{1,0:T(8,128)(2,1)S(1)}, u32[]{:S(2)}, u32[]{:S(2)}) collective-permute-start(bf16[256,1024]{1,0:T(8,128)(2,1)S(1)} %constant_dynamic-update-slice_fusion.2.refs_2_), channel_id=1, source_target_pairs={{0,8},{8,0},{16,24},{24,16},{32,40},{40,32},{48,56},{56,48},{64,72... | collective-permute-start | bytes 1572872 | tf_op jit(solution)/shard_map/ppermute | solution.py:299
  86.3 27.5 %all-to-all-start.1 = ((bf16[16,12,16,128]{3,2,1,0:T(8,128)(2,1)}), bf16[16,12,16,128]{3,2,1,0:T(8,128)(2,1)S(1)}, u32[]{:S(2)}, u32[]{:S(2)}) async-start(bf16[16,12,16,128]{3,2,1,0:T(8,128)(2,1)} %bitcast.8), calls=%async_computation.1 | async-start | bytes 1572864 | tf_op jit(solution)/shard_map/all_to_all | solution.py:275
  91.1 28.3 %collective-permute-start.27 = (bf16[32,16,128]{2,1,0:T(8,128)(2,1)S(1)}, bf16[32,16,128]{2,1,0:T(8,128)(2,1)S(1)}, u32[]{:S(2)}, u32[]{:S(2)}) collective-permute-start(bf16[32,16,128]{2,1,0:T(8,128)(2,1)S(1)} %get-tuple-element.23), channel_id=1, source_target_pairs={{0,7},{1,2},{2,1},{3,4},{4,3},{5,6},{6,5},{7,0},{8,15},{9,10},{10,... | collective-permute-start | bytes 393224 | tf_op jit(solution)/shard_map/ppermute | solution.py:271
  114.6 21.5 %collective-permute-start.16 = (bf16[48,16,128]{2,1,0:T(8,128)(2,1)S(1)}, bf16[48,16,128]{2,1,0:T(8,128)(2,1)}, u32[]{:S(2)}, u32[]{:S(2)}) collective-permute-start(bf16[48,16,128]{2,1,0:T(8,128)(2,1)S(1)} %bitcast.70), channel_id=1, source_target_pairs={{0,7},{1,2},{2,1},{3,4},{4,3},{5,6},{6,5},{7,0},{8,15},{9,10},{10,... | collective-permute-start | bytes 589832 | tf_op jit(solution)/shard_map/ppermute | solution.py:271
  114.6 21.5 %collective-permute-start.17 = (bf16[48,16,128]{2,1,0:T(8,128)(2,1)S(1)}, bf16[48,16,128]{2,1,0:T(8,128)(2,1)}, u32[]{:S(2)}, u32[]{:S(2)}) collective-permute-start(bf16[48,16,128]{2,1,0:T(8,128)(2,1)S(1)} %bitcast.69), channel_id=1, source_target_pairs={{0,2},{1,7},{2,4},{3,1},{4,6},{5,3},{6,0},{7,5},{8,10},{9,15},{10,... | collective-permute-start | bytes 589832 | tf_op jit(solution)/shard_map/ppermute | solution.py:271
  115.8 21.8 %collective-permute-start.18 = (bf16[48,16,128]{2,1,0:T(8,128)(2,1)S(1)}, bf16[48,16,128]{2,1,0:T(8,128)(2,1)}, u32[]{:S(2)}, u32[]{:S(2)}) collective-permute-start(bf16[48,16,128]{2,1,0:T(8,128)(2,1)S(1)} %bitcast.68), channel_id=1, source_target_pairs={{0,5},{1,4},{2,7},{3,6},{4,1},{5,0},{6,3},{7,2},{8,13},{9,12},{10,... | collective-permute-start | bytes 589832 | tf_op jit(solution)/shard_map/ppermute | solution.py:271
  119.4 22.0 %collective-permute-start.29 = (bf16[32,16,128]{2,1,0:T(8,128)(2,1)S(1)}, bf16[32,16,128]{2,1,0:T(8,128)(2,1)S(1)}, u32[]{:S(2)}, u32[]{:S(2)}) collective-permute-start(bf16[32,16,128]{2,1,0:T(8,128)(2,1)S(1)} %get-tuple-element.25), channel_id=1, source_target_pairs={{0,5},{1,4},{2,7},{3,6},{4,1},{5,0},{6,3},{7,2},{8,13},{9,12},{10,... | collective-permute-start | bytes 393224 | tf_op jit(solution)/shard_map/ppermute | solution.py:271
  125.6 22.4 %collective-permute-start.19 = (bf16[48,16,128]{2,1,0:T(8,128)(2,1)}, bf16[48,16,128]{2,1,0:T(8,128)(2,1)}, u32[]{:S(2)}, u32[]{:S(2)}) collective-permute-start(bf16[48,16,128]{2,1,0:T(8,128)(2,1)} %bitcast.10.refs_0_), channel_id=1, source_target_pairs={{0,1},{1,0},{2,3},{3,2},{4,5},{5,4},{6,7},{7,6},{8,9},{9,8},{10,11... | collective-permute-start | bytes 589832 | tf_op jit(solution)/shard_map/ppermute | solution.py:268
  136.1 11.8 %collective-permute-start.20 = (bf16[48,16,128]{2,1,0:T(8,128)(2,1)}, bf16[48,16,128]{2,1,0:T(8,128)(2,1)}, u32[]{:S(2)}, u32[]{:S(2)}) collective-permute-start(bf16[48,16,128]{2,1,0:T(8,128)(2,1)} %collective-permute-done.16.refs_1_), channel_id=1, source_target_pairs={{0,1},{1,0},{2,3},{3,2},{4,5},{5,4},{6,7},{7,6},{8,9},{9,8},{10,11... | collective-permute-start | bytes 589832 | tf_op jit(solution)/shard_map/ppermute | solution.py:268
  136.1 12.1 %collective-permute-start.21 = (bf16[48,16,128]{2,1,0:T(8,128)(2,1)}, bf16[48,16,128]{2,1,0:T(8,128)(2,1)}, u32[]{:S(2)}, u32[]{:S(2)}) collective-permute-start(bf16[48,16,128]{2,1,0:T(8,128)(2,1)} %collective-permute-done.17.refs_2_), channel_id=1, source_target_pairs={{0,1},{1,0},{2,3},{3,2},{4,5},{5,4},{6,7},{7,6},{8,9},{9,8},{10,11... | collective-permute-start | bytes 589832 | tf_op jit(solution)/shard_map/ppermute | solution.py:268
  137.6 13.1 %collective-permute-start.22 = (bf16[48,16,128]{2,1,0:T(8,128)(2,1)}, bf16[48,16,128]{2,1,0:T(8,128)(2,1)}, u32[]{:S(2)}, u32[]{:S(2)}) collective-permute-start(bf16[48,16,128]{2,1,0:T(8,128)(2,1)} %collective-permute-done.18.refs_3_), channel_id=1, source_target_pairs={{0,1},{1,0},{2,3},{3,2},{4,5},{5,4},{6,7},{7,6},{8,9},{9,8},{10,11... | collective-permute-start | bytes 589832 | tf_op jit(solution)/shard_map/ppermute | solution.py:268
  143.4 22.6 %all-to-all-start.3 = ((bf16[16,8,16,128]{3,2,1,0:T(8,128)(2,1)}), bf16[16,8,16,128]{3,2,1,0:T(8,128)(2,1)S(1)}, u32[]{:S(2)}, u32[]{:S(2)}) async-start(bf16[16,8,16,128]{3,2,1,0:T(8,128)(2,1)} %bitcast.65), calls=%async_computation.3 | async-start | bytes 1048576 | tf_op jit(solution)/shard_map/all_to_all | solution.py:275
  164.5 19.5 %collective-permute-start.23 = (bf16[192,16,128]{2,1,0:T(8,128)(2,1)}, bf16[192,16,128]{2,1,0:T(8,128)(2,1)}, u32[]{:S(2)}, u32[]{:S(2)}) collective-permute-start(bf16[192,16,128]{2,1,0:T(8,128)(2,1)} %get-tuple-element.21), channel_id=1, source_target_pairs={{0,1},{1,0},{2,3},{3,2},{4,5},{5,4},{6,7},{7,6},{8,9},{9,8},{10,11... | collective-permute-start | bytes 2359304 | tf_op jit(solution)/shard_map/ppermute | solution.py:268
  165.9 29.2 %collective-permute-start.30 = (bf16[128,16,128]{2,1,0:T(8,128)(2,1)S(1)}, bf16[128,16,128]{2,1,0:T(8,128)(2,1)}, u32[]{:S(2)}, u32[]{:S(2)}) collective-permute-start(bf16[128,16,128]{2,1,0:T(8,128)(2,1)S(1)} %bitcast.57), channel_id=1, source_target_pairs={{0,1},{1,0},{2,3},{3,2},{4,5},{5,4},{6,7},{7,6},{8,9},{9,8},{10,11... | collective-permute-start | bytes 1572872 | tf_op jit(solution)/shard_map/ppermute | solution.py:268
  186.4 41.2 %all-to-all-start.2 = ((bf16[16,12,16,128]{3,2,1,0:T(8,128)(2,1)}), bf16[16,12,16,128]{3,2,1,0:T(8,128)(2,1)}, u32[]{:S(2)}, u32[]{:S(2)}) async-start(bf16[16,12,16,128]{3,2,1,0:T(8,128)(2,1)} %bitcast.64), calls=%async_computation.2 | async-start | bytes 1572864 | tf_op jit(solution)/shard_map/all_to_all | solution.py:275
  204.0 10.7 %collective-permute-start.32 = (bf16[96,16,128]{2,1,0:T(8,128)(2,1)S(1)}, bf16[96,16,128]{2,1,0:T(8,128)(2,1)S(1)}, u32[]{:S(2)}, u32[]{:S(2)}) collective-permute-start(bf16[96,16,128]{2,1,0:T(8,128)(2,1)S(1)} %get-tuple-element.29), channel_id=1, source_target_pairs={{0,1},{1,0},{2,3},{3,2},{4,5},{5,4},{6,7},{7,6},{8,9},{9,8},{10,11... | collective-permute-start | bytes 1179656 | tf_op jit(solution)/shard_map/ppermute | solution.py:268
  205.8 13.8 %collective-permute-start.31 = (bf16[32,16,128]{2,1,0:T(8,128)(2,1)S(1)}, bf16[32,16,128]{2,1,0:T(8,128)(2,1)S(1)}, u32[]{:S(2)}, u32[]{:S(2)}) collective-permute-start(bf16[32,16,128]{2,1,0:T(8,128)(2,1)S(1)} %get-tuple-element.27), channel_id=1, source_target_pairs={{0,1},{1,0},{2,3},{3,2},{4,5},{5,4},{6,7},{7,6},{8,9},{9,8},{10,11... | collective-permute-start | bytes 393224 | tf_op jit(solution)/shard_map/ppermute | solution.py:268
  217.2 9.5 %collective-permute-start.35 = (bf16[32,16,128]{2,1,0:T(8,128)(2,1)S(1)}, bf16[32,16,128]{2,1,0:T(8,128)(2,1)S(1)}, u32[]{:S(2)}, u32[]{:S(2)}) collective-permute-start(bf16[32,16,128]{2,1,0:T(8,128)(2,1)S(1)} %get-tuple-element.45), channel_id=1, source_target_pairs={{5,0},{4,1},{7,2},{6,3},{1,4},{0,5},{3,6},{2,7},{13,8},{12,9},{15,... | collective-permute-start | bytes 393224 | tf_op jit(solution)/shard_map/ppermute | solution.py:271
  227.6 28.0 %all-to-all-start.4 = ((bf16[16,8,16,128]{3,2,1,0:T(8,128)(2,1)}), bf16[16,8,16,128]{3,2,1,0:T(8,128)(2,1)S(1)}, u32[]{:S(2)}, u32[]{:S(2)}) async-start(bf16[16,8,16,128]{3,2,1,0:T(8,128)(2,1)} %bitcast.30), calls=%async_computation.4 | async-start | bytes 1048576 | tf_op jit(solution)/shard_map/all_to_all | solution.py:275
  239.8 15.9 %collective-permute-start.24 = (bf16[48,16,128]{2,1,0:T(8,128)(2,1)S(1)}, bf16[48,16,128]{2,1,0:T(8,128)(2,1)S(1)}, u32[]{:S(2)}, u32[]{:S(2)}) collective-permute-start(bf16[48,16,128]{2,1,0:T(8,128)(2,1)S(1)} %bitcast.73), channel_id=1, source_target_pairs={{7,0},{2,1},{1,2},{4,3},{3,4},{6,5},{5,6},{0,7},{15,8},{10,9},{9,1... | collective-permute-start | bytes 589832 | tf_op jit(solution)/shard_map/ppermute | solution.py:271
  241.3 14.4 %collective-permute-start.25 = (bf16[48,16,128]{2,1,0:T(8,128)(2,1)S(1)}, bf16[48,16,128]{2,1,0:T(8,128)(2,1)S(1)}, u32[]{:S(2)}, u32[]{:S(2)}) collective-permute-start(bf16[48,16,128]{2,1,0:T(8,128)(2,1)S(1)} %bitcast.72), channel_id=1, source_target_pairs={{2,0},{7,1},{4,2},{1,3},{6,4},{3,5},{0,6},{5,7},{10,8},{15,9},{12,... | collective-permute-start | bytes 589832 | tf_op jit(solution)/shard_map/ppermute | solution.py:271
  242.2 15.7 %collective-permute-start.26 = (bf16[48,16,128]{2,1,0:T(8,128)(2,1)S(1)}, bf16[48,16,128]{2,1,0:T(8,128)(2,1)S(1)}, u32[]{:S(2)}, u32[]{:S(2)}) collective-permute-start(bf16[48,16,128]{2,1,0:T(8,128)(2,1)S(1)} %bitcast.71), channel_id=1, source_target_pairs={{5,0},{4,1},{7,2},{6,3},{1,4},{0,5},{3,6},{2,7},{13,8},{12,9},{15,... | collective-permute-start | bytes 589832 | tf_op jit(solution)/shard_map/ppermute | solution.py:271
  (21 other events, 261.1 us)

commit v2 on v1

--- a/solution.py
+++ b/solution.py
@@ -138,8 +138,16 @@
 
 
 def experts_kernel(count, turns, moves, *refs):
-    ins, (gate_up, down), outs = refs[:count], refs[count : count + 2], refs[count + 2 : -4]
-    lhs, tiles, both, hidden = refs[-4:]
+    ins, (gate_up_far, down_far), outs = refs[:count], refs[count : count + 2], refs[count + 2 : -7]
+    lhs, tiles, both, hidden, gate_up, down, arrived = refs[-7:]
+
+    def fetch(k):
+        return pltpu.make_async_copy(gate_up_far.at[0, k], gate_up.at[k], arrived.at[k])
+
+    fetch_down = pltpu.make_async_copy(down_far.at[0], down, arrived.at[2])
+    fetch(0).start()
+    fetch(1).start()
+    fetch_down.start()
     rows, wide = lhs.shape
     chunks = wide // LANES
     group = 16
@@ -165,16 +173,18 @@
     lax.fori_loop(0, rows // group, spread_lanes, 0)
 
     def project_up(k, carry):
-        both[k] = dot_t(gate_up[0, k], lhs[...])
+        fetch(k).wait()
+        both[k] = dot_t(gate_up[k], lhs[...])
         return carry
 
     lax.fori_loop(0, 2, project_up, 0)
     gate = both[0]
     hidden[...] = (gate / (1.0 + jnp.exp(-gate)) * both[1]).T.astype(jnp.bfloat16)
     step = wide // 4
+    fetch_down.wait()
 
     def project_down(n, carry):
-        part = down[0, :, pl.ds(pl.multiple_of(n * step, step), step)]
+        part = down[:, pl.ds(pl.multiple_of(n * step, step), step)]
         made = jnp.dot(hidden[...], part, preferred_element_type=jnp.float32)
         for c in range(step // LANES):
             tiles[pl.ds(n * (step // LANES) + c, rows, stride=chunks), :] = made[:, c * LANES : (c + 1) * LANES]
@@ -197,7 +207,7 @@
     rows, wide, units = sum(b.shape[0] for b in ins), chunks * LANES, w_down.shape[1]
     return pl.pallas_call(
         functools.partial(experts_kernel, len(ins), turns, moves),
-        in_specs=[whole(VMEM)] * (len(ins) + 2),
+        in_specs=[whole(VMEM)] * len(ins) + [whole(pltpu.HBM)] * 2,
         out_specs=[whole(VMEM)] * len(sizes),
         out_shape=[jax.ShapeDtypeStruct((n, chunks, LANES), jnp.bfloat16) for n in sizes],
         scratch_shapes=[
@@ -205,8 +215,11 @@
             VMEM((rows * chunks, LANES), jnp.float32),
             VMEM((2, units, rows), jnp.float32),
             VMEM((rows, units), jnp.bfloat16),
+            VMEM(w_gate_up.shape[1:], jnp.bfloat16),
+            VMEM(w_down.shape[1:], jnp.bfloat16),
+            pltpu.SemaphoreType.DMA((3,)),
         ],
-        compiler_params=pltpu.CompilerParams(vmem_limit_bytes=2 * LIMIT),
+        compiler_params=pltpu.CompilerParams(vmem_limit_bytes=52 << 20),
         cost_estimate=pl.CostEstimate(
             flops=6 * rows * wide * units, bytes_accessed=6 * units * wide, transcendentals=rows * units
         ),
@@ -326,11 +339,7 @@
     index_out = jnp.where(early, by_column * cap_a + places, first + by_message * cap_b + places - cap_a)
     index_in = jnp.where(early, by_message * cap_a + places, first + by_column * cap_b + places - cap_a)
     index_out, index_in = index_out.astype(jnp.int32), index_in.astype(jnp.int32)
-    moves_a = tuple(
-        (d, m * cap_a, group * cap_a, (d * group + m) * columns * cap_a, cap_a, cap_a)
-        for d in range(2)
-        for m in range(group)
-    )
+    moves_a = tuple((0, m * cap_a, group * cap_a, m * columns * cap_a, cap_a, cap_a) for m in range(group))
     moves_b = tuple(
         (2 * d + (m > 0), max(m - 1, 0) * columns * cap_b, cap_b, (d * lines + m) * cap_b, group * cap_b, cap_b)
         for d in range(2)
@@ -355,10 +364,12 @@
     near_b = spread(boxes_b, out_hops)
     near_b = across(join(near_b))
     near_a = spread(split(over_a), out_hops)
-    far_a = [swapped(b) for b in near_a]
+    far_a = [swapped(near_a[0])]
+    far_a += [swapped(b) for b in near_a[1:]]
     far_b = swapped(near_b)
 
-    own_a, other_a = run_experts(near_a + far_a, w_gate_up, w_down, columns, moves_a, [lines * cap_a] * 2)
+    (own_a,) = run_experts(near_a, w_gate_up, w_down, columns, moves_a, [lines * cap_a])
+    (other_a,) = run_experts(far_a, w_gate_up, w_down, columns, moves_a, [lines * cap_a])
     sum_a = add_halves(own_a, swapped(other_a))
     few = columns * cap_b
     made_b = run_experts([near_b, far_b], w_gate_up, w_down, columns, moves_b, [few, (group - 1) * few] * 2)

time: 263 us -> 247 us (0.939)
  local copies, waits for them, and re-layouts: 16.1 us -> 8 us
  starting transfers between devices: 95.7 us -> 90.7 us
    unnamed x32 -> x16, local copies, waits for them, and re-layouts: 8.26 us -> 2.07 us
    ppermute x11, waiting for transfers between devices: 33.5 us -> 37.2 us  [swapped(): return lax.ppermute(value, 'fsdp', swap)]
    ppermute x12, waiting for transfers between devices: 22.6 us -> 19.2 us  [spread(): lax.ppermute(b, 'fsdp', hop)]
    pallas_call x2 -> x3, Pallas kernels: 16.4 us -> 18.5 us  [run_experts(): pl.pallas_call(functools.partial(experts_kernel, len(ins), turns, moves),...]
  transfers between devices with their start and end apart: 40 -> 40, of which waited for: 16 -> 17; matrix products, arithmetic and copies ran while one was open for 5% -> 4% of each run, Pallas kernels for 7% -> 9%
where the time goes in v2:
time: 247 us; the launch traced here: 246 us
  waiting for transfers between devices  96.9 us (39%)
  starting transfers between devices  90.7 us (37%)
  Pallas kernels  30 us (12%)
  blocking collectives  17 us (7%)
  local copies, waits for them, and re-layouts  8 us (3%)
  other arithmetic  3.3 us (1%)
    ppermute x11, waiting for transfers between devices, swapped(): return lax.ppermute(value, 'fsdp', swap)  37.2 us
    all_to_all x4, waiting for transfers between devices, across(): lax.all_to_all(boxes, 'expert', split_axis=0, concat_axis=0, tiled=True)  31.5 us
    all_to_all x4, starting transfers between devices, across(): lax.all_to_all(boxes, 'expert', split_axis=0, concat_axis=0, tiled=True)  26.8 us
    ppermute x8, starting transfers between devices, on_device(): lax.ppermute(value, 'expert', [(i, (i + by) % columns) for i in range(col...  21.1 us
    ppermute x12, waiting for transfers between devices, spread(): lax.ppermute(b, 'fsdp', hop)  19.2 us
    pallas_call x3, Pallas kernels, run_experts(): pl.pallas_call(functools.partial(experts_kernel, len(ins), turns, moves),...  18.5 us
    all_to_all x1, blocking collectives, on_device(): lax.all_to_all(pieces, 'fsdp', split_axis=0, concat_axis=0, tiled=True)  17 us
    ppermute x5, starting transfers between devices, on_device(): lax.ppermute(value, 'expert', [(i, i ^ 1) for i in range(columns)])  16.7 us
  transfers between devices with their start and end apart: 40, of which 17 were waited for; matrix products, arithmetic and copies ran while one was open for 4% of the time, Pallas kernels for 9%

profile of v2, /device:TPU:513, one launch (start us, length us, event | category | flops | bytes accessed | tf_op | source)
XLA Modules:
  0.0 246.3 jit_solution(11147873520273943730)
XLA Ops:
  0.9 17.0 %all_to_all.25 = bf16[8,16,1024]{2,1,0:T(8,128)(2,1)S(1)} all-to-all(bf16[8,16,1024]{2,1,0:T(8,128)(2,1)S(1)} %bitcast.67), channel_id=1, replica_groups=mesh['sweep'=2,'expert'=16,'fsdp'=8] {'fsdp'}, dimensions={0} | all-to-all | bytes 524288 | tf_op jit(solution)/shard_map/all_to_all | solution.py:309
  17.9 3.8 %collective-permute-start = (bf16[128,1024]{1,0:T(8,128)(2,1)S(1)}, bf16[128,1024]{1,0:T(8,128)(2,1)S(1)}, u32[]{:S(2)}, u32[]{:S(2)}) collective-permute-start(bf16[128,1024]{1,0:T(8,128)(2,1)S(1)} %bitcast.52), channel_id=1, source_target_pairs={{0,16},{8,24},{16,32},{24,40},{32,48},{40,56},{48,64},{56,72},{64,... | collective-permute-start | bytes 786440 | tf_op jit(solution)/shard_map/ppermute | solution.py:311
  21.6 9.1 %collective-permute-start.1 = (bf16[128,1024]{1,0:T(8,128)(2,1)S(1)}, bf16[128,1024]{1,0:T(8,128)(2,1)S(1)}, u32[]{:S(2)}, u32[]{:S(2)}) collective-permute-start(bf16[128,1024]{1,0:T(8,128)(2,1)S(1)} %bitcast.53), channel_id=1, source_target_pairs={{0,112},{8,120},{16,0},{24,8},{32,16},{40,24},{48,32},{56,40},{64,... | collective-permute-start | bytes 786440 | tf_op jit(solution)/shard_map/ppermute | solution.py:311
  30.7 3.8 %collective-permute-done = bf16[128,1024]{1,0:T(8,128)(2,1)S(1)} collective-permute-done((bf16[128,1024]{1,0:T(8,128)(2,1)S(1)}, bf16[128,1024]{1,0:T(8,128)(2,1)S(1)}, u32[]{:S(2)}, u32[]{:S(2)}) %collective-permute-start) | collective-permute-done | bytes 262176 | tf_op jit(solution)/shard_map/ppermute | solution.py:311
  34.5 2.7 %collective-permute-start.3 = (bf16[128,1024]{1,0:T(8,128)(2,1)S(1)}, bf16[128,1024]{1,0:T(8,128)(2,1)S(1)}, u32[]{:S(2)}, u32[]{:S(2)}) collective-permute-start(bf16[128,1024]{1,0:T(8,128)(2,1)S(1)} %collective-permute-done.1), channel_id=1, source_target_pairs={{0,112},{8,120},{16,0},{24,8},{32,16},{40,24},{48,32},{56,40},{64,... | collective-permute-start | bytes 786440 | tf_op jit(solution)/shard_map/ppermute | solution.py:311
  40.8 3.1 %collective-permute-done.2 = bf16[128,1024]{1,0:T(8,128)(2,1)S(1)} collective-permute-done((bf16[128,1024]{1,0:T(8,128)(2,1)S(1)}, bf16[128,1024]{1,0:T(8,128)(2,1)S(1)}, u32[]{:S(2)}, u32[]{:S(2)}) %collective-permute-start.2) | collective-permute-done | bytes 262176 | tf_op jit(solution)/shard_map/ppermute | solution.py:311
  43.9 2.7 %collective-permute-start.5 = (bf16[128,1024]{1,0:T(8,128)(2,1)S(1)}, bf16[128,1024]{1,0:T(8,128)(2,1)S(1)}, u32[]{:S(2)}, u32[]{:S(2)}) collective-permute-start(bf16[128,1024]{1,0:T(8,128)(2,1)S(1)} %collective-permute-done.3), channel_id=1, source_target_pairs={{0,112},{8,120},{16,0},{24,8},{32,16},{40,24},{48,32},{56,40},{64,... | collective-permute-start | bytes 786440 | tf_op jit(solution)/shard_map/ppermute | solution.py:311
  46.5 10.6 %collective-permute-start.9 = (bf16[256,1024]{1,0:T(8,128)(2,1)S(1)}, bf16[256,1024]{1,0:T(8,128)(2,1)S(1)}, u32[]{:S(2)}, u32[]{:S(2)}) collective-permute-start(bf16[256,1024]{1,0:T(8,128)(2,1)S(1)} %constant_dynamic-update-slice_fusion.refs_1_), channel_id=1, source_target_pairs={{0,8},{8,0},{16,24},{24,16},{32,40},{40,32},{48,56},{56,48},{64,72... | collective-permute-start | bytes 1572872 | tf_op jit(solution)/shard_map/ppermute | solution.py:312
  57.4 2.8 %collective-permute-start.7 = (bf16[64,1024]{1,0:T(8,128)(2,1)S(1)}, bf16[64,1024]{1,0:T(8,128)(2,1)S(1)}, u32[]{:S(2)}, u32[]{:S(2)}) collective-permute-start(bf16[64,1024]{1,0:T(8,128)(2,1)S(1)} %slice.70), channel_id=1, source_target_pairs={{0,112},{8,120},{16,0},{24,8},{32,16},{40,24},{48,32},{56,40},{64,... | collective-permute-start | bytes 393224 | tf_op jit(solution)/shard_map/ppermute | solution.py:311
  62.4 5.3 %collective-permute-start.10 = (bf16[256,1024]{1,0:T(8,128)(2,1)S(1)}, bf16[256,1024]{1,0:T(8,128)(2,1)S(1)}, u32[]{:S(2)}, u32[]{:S(2)}) collective-permute-start(bf16[256,1024]{1,0:T(8,128)(2,1)S(1)} %constant_dynamic-update-slice_fusion.2.refs_2_), channel_id=1, source_target_pairs={{0,8},{8,0},{16,24},{24,16},{32,40},{40,32},{48,56},{56,48},{64,72... | collective-permute-start | bytes 1572872 | tf_op jit(solution)/shard_map/ppermute | solution.py:312
  72.2 3.1 %shard_map.83 = bf16[128,1024]{1,0:T(8,128)(2,1)S(1)} custom-call(s32[1]{0:T(128)} %bitcast.2.position, bf16[128,2048]{1,0:T(8,128)(2,1)} %collective-permute-done.13.context, bf16[128,1024]{1,0:T(8,128)(2,1)} %collective-permute-done.14.tokens, bf16[128,1024]{1,0:T(8,128)(2,1)S(1)} %bitcast.55, ...), custom_call_target="tpu_custom_call" | custom-call | flops 536870912 | bytes 262144 | tf_op jit(solution)/shard_map/pallas_call | solution.py:57
  75.5 2.8 %shard_map.82.mine = bf16[128,1024]{1,0:T(8,128)(2,1)S(1)} custom-call(s32[1]{0:T(128)} %bitcast.2.position, bf16[128,2048]{1,0:T(8,128)(2,1)S(1)} %copy-done.2, bf16[128,1024]{1,0:T(8,128)(2,1)S(1)} %copy-done, bf16[128,1024]{1,0:T(8,128)(2,1)S(1)} %bitcast.56, bf16[256,1024]{1,0:T(8,128)(2,1)S(1)} %constant_dynamic-update-slice_fusion.refs_1_, ...), custom_call_target="tpu_custom_call" | custom-call | flops 536870912 | bytes 262144 | tf_op jit(solution)/shard_map/pallas_call | solution.py:57
  78.3 4.8 %collective-permute-done.15.other = bf16[128,1024]{1,0:T(8,128)(2,1)S(1)} collective-permute-done((bf16[128,1024]{1,0:T(8,128)(2,1)S(1)}, bf16[128,1024]{1,0:T(8,128)(2,1)S(1)}, u32[]{:S(2)}, u32[]{:S(2)}) %collective-permute-start.15) | collective-permute-done | bytes 262176 | tf_op jit(solution)/shard_map/ppermute | solution.py:281
  83.1 3.2 %shard_map.84 = (bf16[192,16,128]{2,1,0:T(8,128)(2,1)}, bf16[32,16,128]{2,1,0:T(8,128)(2,1)S(1)}, bf16[32,16,128]{2,1,0:T(8,128)(2,1)S(1)}, bf16[32,16,128]{2,1,...) custom-call(s32[256]{0:T(256)S(1)} %get-tuple-element.27.index, ...), custom_call_target="tpu_custom_call" | custom-call | flops 16777216 | bytes 8388608 | tf_op jit(solution)/shard_map/pallas_call | solution.py:124
  86.3 4.8 %all-to-all-start.1 = ((bf16[16,12,16,128]{3,2,1,0:T(8,128)(2,1)}), bf16[16,12,16,128]{3,2,1,0:T(8,128)(2,1)S(1)}, u32[]{:S(2)}, u32[]{:S(2)}) async-start(bf16[16,12,16,128]{3,2,1,0:T(8,128)(2,1)} %bitcast.8), calls=%async_computation.1 | async-start | bytes 1572864 | tf_op jit(solution)/shard_map/all_to_all | solution.py:288
  94.1 19.7 %all-to-all-done.1 = bf16[16,12,16,128]{3,2,1,0:T(8,128)(2,1)S(1)} async-done(((bf16[16,12,16,128]{3,2,1,0:T(8,128)(2,1)}), bf16[16,12,16,128]{3,2,1,0:T(8,128)(2,1)S(1)}, u32[]{:S(2)}, u32[]{:S(2)}) %all-to-all-start.1) | async-done | bytes 786464 | tf_op jit(solution)/shard_map/all_to_all | solution.py:288
  118.0 3.9 %all-to-all-start.3 = ((bf16[16,8,16,128]{3,2,1,0:T(8,128)(2,1)}), bf16[16,8,16,128]{3,2,1,0:T(8,128)(2,1)S(1)}, u32[]{:S(2)}, u32[]{:S(2)}) async-start(bf16[16,8,16,128]{3,2,1,0:T(8,128)(2,1)} %bitcast.24), calls=%async_computation.3 | async-start | bytes 1048576 | tf_op jit(solution)/shard_map/all_to_all | solution.py:288
  122.7 7.4 %collective-permute-done.16.refs_1_ = bf16[48,16,128]{2,1,0:T(8,128)(2,1)S(1)} collective-permute-done((bf16[48,16,128]{2,1,0:T(8,128)(2,1)S(1)}, bf16[48,16,128]{2,1,0:T(8,128)(2,1)S(1)}, u32[]{:S(2)}, u32[]{:S(2)}) %collective-permute-start.16) | collective-permute-done | bytes 196640 | tf_op jit(solution)/shard_map/ppermute | solution.py:284
  133.8 3.3 %collective-permute-done.20.refs_1_ = bf16[48,16,128]{2,1,0:T(8,128)(2,1)S(1)} collective-permute-done((bf16[48,16,128]{2,1,0:T(8,128)(2,1)S(1)}, bf16[48,16,128]{2,1,0:T(8,128)(2,1)S(1)}, u32[]{:S(2)}, u32[]{:S(2)}) %collective-permute-start.20) | collective-permute-done | bytes 196640 | tf_op jit(solution)/shard_map/ppermute | solution.py:281
  137.1 4.2 %collective-permute-done.21.refs_2_ = bf16[48,16,128]{2,1,0:T(8,128)(2,1)S(1)} collective-permute-done((bf16[48,16,128]{2,1,0:T(8,128)(2,1)S(1)}, bf16[48,16,128]{2,1,0:T(8,128)(2,1)S(1)}, u32[]{:S(2)}, u32[]{:S(2)}) %collective-permute-start.21) | collective-permute-done | bytes 196640 | tf_op jit(solution)/shard_map/ppermute | solution.py:281
  141.3 3.1 %collective-permute-done.22.refs_3_ = bf16[48,16,128]{2,1,0:T(8,128)(2,1)S(1)} collective-permute-done((bf16[48,16,128]{2,1,0:T(8,128)(2,1)S(1)}, bf16[48,16,128]{2,1,0:T(8,128)(2,1)S(1)}, u32[]{:S(2)}, u32[]{:S(2)}) %collective-permute-start.22) | collective-permute-done | bytes 196640 | tf_op jit(solution)/shard_map/ppermute | solution.py:281
  144.3 5.7 %shard_map.86 = bf16[192,16,128]{2,1,0:T(8,128)(2,1)S(1)} custom-call(bf16[48,16,128]{2,1,0:T(8,128)(2,1)S(1)} %collective-permute-done.19.refs_0_, bf16[48,16,128]{2,1,0:T(8,128)(2,1)S(1)} %collective-permute-done.20.refs_1_, bf16[48,16,128]{2,1,0:T(8,128)(2,1)S(1)} %collective-permute-done.21.refs_2_, ...), custom_call_target="tpu_custom_call" | custom-call | flops 1660944384 | bytes 8650752 | tf_op jit(solution)/shard_map/pallas_call | solution.py:208
  152.4 5.7 %shard_map.85 = bf16[192,16,128]{2,1,0:T(8,128)(2,1)S(1)} custom-call(bf16[48,16,128]{2,1,0:T(8,128)(2,1)S(1)} %bitcast.61, bf16[48,16,128]{2,1,0:T(8,128)(2,1)S(1)} %collective-permute-done.16.refs_1_, bf16[48,16,128]{2,1,0:T(8,128)(2,1)S(1)} %collective-permute-done.17.refs_2_, bf16[48,16,128]{2,1,0:T(8,128)(2,1)S(1)} %collective-permute-done.18.refs_3_, ...), custom_call_target="tpu_custom_call" | custom-call | flops 1660944384 | bytes 8650752 | tf_op jit(solution)/shard_map/pallas_call | solution.py:208
  158.1 12.1 %collective-permute-done.23 = bf16[192,16,128]{2,1,0:T(8,128)(2,1)} collective-permute-done((bf16[192,16,128]{2,1,0:T(8,128)(2,1)S(1)}, bf16[192,16,128]{2,1,0:T(8,128)(2,1)}, u32[]{:S(2)}, u32[]{:S(2)}) %collective-permute-start.23) | collective-permute-done | bytes 786464 | tf_op jit(solution)/shard_map/ppermute | solution.py:281
  172.5 7.9 %all-to-all-start.2 = ((bf16[16,12,16,128]{3,2,1,0:T(8,128)(2,1)}), bf16[16,12,16,128]{3,2,1,0:T(8,128)(2,1)S(1)}, u32[]{:S(2)}, u32[]{:S(2)}) async-start(bf16[16,12,16,128]{3,2,1,0:T(8,128)(2,1)} %bitcast.14), calls=%async_computation.2 | async-start | bytes 1572864 | tf_op jit(solution)/shard_map/all_to_all | solution.py:288
  181.5 7.1 %shard_map.87 = (bf16[32,16,128]{2,1,0:T(8,128)(2,1)S(1)}, bf16[96,16,128]{2,1,0:T(8,128)(2,1)S(1)}, bf16[32,16,128]{2,1,0:T(8,128)(2,1)S(1)}, bf16[96,16,128]{2,1,0:T(8,128)(2,1)S(1)}) custom-call(bf16[128,16,128]{2,1,0:T(8,128)(2,1)S(1)} %bitcast.58, bf16[128,16,128]{2,1,0:T(8,128)(2,1)} %collective-permute-done.30.refs_1_, ...), custom_call_target="tpu_custom_call" | custom-call | flops 2214592512 | bytes 8650752 | tf_op jit(solution)/shard_map/pallas_call | solution.py:208
  190.2 8.6 %collective-permute-done.32 = bf16[96,16,128]{2,1,0:T(8,128)(2,1)S(1)} collective-permute-done((bf16[96,16,128]{2,1,0:T(8,128)(2,1)S(1)}, bf16[96,16,128]{2,1,0:T(8,128)(2,1)S(1)}, u32[]{:S(2)}, u32[]{:S(2)}) %collective-permute-start.32) | collective-permute-done | bytes 393248 | tf_op jit(solution)/shard_map/ppermute | solution.py:281
  200.7 3.1 %collective-permute-start.35 = (bf16[32,16,128]{2,1,0:T(8,128)(2,1)S(1)}, bf16[32,16,128]{2,1,0:T(8,128)(2,1)S(1)}, u32[]{:S(2)}, u32[]{:S(2)}) collective-permute-start(bf16[32,16,128]{2,1,0:T(8,128)(2,1)S(1)} %get-tuple-element.41), channel_id=1, source_target_pairs={{5,0},{4,1},{7,2},{6,3},{1,4},{0,5},{3,6},{2,7},{13,8},{12,9},{15,... | collective-permute-start | bytes 393224 | tf_op jit(solution)/shard_map/ppermute | solution.py:284
  204.9 5.4 %collective-permute-done.35 = bf16[32,16,128]{2,1,0:T(8,128)(2,1)S(1)} collective-permute-done((bf16[32,16,128]{2,1,0:T(8,128)(2,1)S(1)}, bf16[32,16,128]{2,1,0:T(8,128)(2,1)S(1)}, u32[]{:S(2)}, u32[]{:S(2)}) %collective-permute-start.35) | collective-permute-done | bytes 131104 | tf_op jit(solution)/shard_map/ppermute | solution.py:284
  211.2 10.2 %all-to-all-start.4 = ((bf16[16,8,16,128]{3,2,1,0:T(8,128)(2,1)}), bf16[16,8,16,128]{3,2,1,0:T(8,128)(2,1)S(1)}, u32[]{:S(2)}, u32[]{:S(2)}) async-start(bf16[16,8,16,128]{3,2,1,0:T(8,128)(2,1)} %bitcast.30), calls=%async_computation.4 | async-start | bytes 1048576 | tf_op jit(solution)/shard_map/all_to_all | solution.py:288
  226.7 11.8 %all-to-all-done.4 = bf16[16,8,16,128]{3,2,1,0:T(8,128)(2,1)S(1)} async-done(((bf16[16,8,16,128]{3,2,1,0:T(8,128)(2,1)}), bf16[16,8,16,128]{3,2,1,0:T(8,128)(2,1)S(1)}, u32[]{:S(2)}, u32[]{:S(2)}) %all-to-all-start.4) | async-done | bytes 524320 | tf_op jit(solution)/shard_map/all_to_all | solution.py:288
  238.5 5.4 %collective-permute-done.26.refs_3_ = bf16[48,16,128]{2,1,0:T(8,128)(2,1)S(1)} collective-permute-done((bf16[48,16,128]{2,1,0:T(8,128)(2,1)S(1)}, bf16[48,16,128]{2,1,0:T(8,128)(2,1)S(1)}, u32[]{:S(2)}, u32[]{:S(2)}) %collective-permute-start.26) | collective-permute-done | bytes 196640 | tf_op jit(solution)/shard_map/ppermute | solution.py:284
  (103 shorter events, 42.0 us)
Async XLA Ops:
  17.9 16.6 %collective-permute-start = (bf16[128,1024]{1,0:T(8,128)(2,1)S(1)}, bf16[128,1024]{1,0:T(8,128)(2,1)S(1)}, u32[]{:S(2)}, u32[]{:S(2)}) collective-permute-start(bf16[128,1024]{1,0:T(8,128)(2,1)S(1)} %bitcast.52), channel_id=1, source_target_pairs={{0,16},{8,24},{16,32},{24,40},{32,48},{40,56},{48,64},{56,72},{64,... | collective-permute-start | bytes 786440 | tf_op jit(solution)/shard_map/ppermute | solution.py:311
  21.6 12.9 %collective-permute-start.1 = (bf16[128,1024]{1,0:T(8,128)(2,1)S(1)}, bf16[128,1024]{1,0:T(8,128)(2,1)S(1)}, u32[]{:S(2)}, u32[]{:S(2)}) collective-permute-start(bf16[128,1024]{1,0:T(8,128)(2,1)S(1)} %bitcast.53), channel_id=1, source_target_pairs={{0,112},{8,120},{16,0},{24,8},{32,16},{40,24},{48,32},{56,40},{64,... | collective-permute-start | bytes 786440 | tf_op jit(solution)/shard_map/ppermute | solution.py:311
  34.5 9.4 %collective-permute-start.2 = (bf16[128,1024]{1,0:T(8,128)(2,1)S(1)}, bf16[128,1024]{1,0:T(8,128)(2,1)S(1)}, u32[]{:S(2)}, u32[]{:S(2)}) collective-permute-start(bf16[128,1024]{1,0:T(8,128)(2,1)S(1)} %collective-permute-done), channel_id=1, source_target_pairs={{0,16},{8,24},{16,32},{24,40},{32,48},{40,56},{48,64},{56,72},{64,... | collective-permute-start | bytes 786440 | tf_op jit(solution)/shard_map/ppermute | solution.py:311
  34.5 9.4 %collective-permute-start.3 = (bf16[128,1024]{1,0:T(8,128)(2,1)S(1)}, bf16[128,1024]{1,0:T(8,128)(2,1)S(1)}, u32[]{:S(2)}, u32[]{:S(2)}) collective-permute-start(bf16[128,1024]{1,0:T(8,128)(2,1)S(1)} %collective-permute-done.1), channel_id=1, source_target_pairs={{0,112},{8,120},{16,0},{24,8},{32,16},{40,24},{48,32},{56,40},{64,... | collective-permute-start | bytes 786440 | tf_op jit(solution)/shard_map/ppermute | solution.py:311
  39.0 30.0 %collective-permute-start.14 = (bf16[128,1024]{1,0:T(8,128)(2,1)}, bf16[128,1024]{1,0:T(8,128)(2,1)}, u32[]{:S(2)}, u32[]{:S(2)}) collective-permute-start(bf16[128,1024]{1,0:T(8,128)(2,1)} %get-tuple-element.38), channel_id=1, source_target_pairs={{0,1},{1,0},{2,3},{3,2},{4,5},{5,4},{6,7},{7,6},{8,9},{9,8},{10,11... | collective-permute-start | bytes 786440 | tf_op jit(solution)/shard_map/ppermute | solution.py:281
  39.0 30.5 %collective-permute-start.13 = (bf16[128,2048]{1,0:T(8,128)(2,1)S(1)}, bf16[128,2048]{1,0:T(8,128)(2,1)}, u32[]{:S(2)}, u32[]{:S(2)}) collective-permute-start(bf16[128,2048]{1,0:T(8,128)(2,1)S(1)} %copy-done.1), channel_id=1, source_target_pairs={{0,1},{1,0},{2,3},{3,2},{4,5},{5,4},{6,7},{7,6},{8,9},{9,8},{10,11... | collective-permute-start | bytes 1572872 | tf_op jit(solution)/shard_map/ppermute | solution.py:281
  43.8 13.4 %collective-permute-start.4 = (bf16[128,1024]{1,0:T(8,128)(2,1)S(1)}, bf16[128,1024]{1,0:T(8,128)(2,1)S(1)}, u32[]{:S(2)}, u32[]{:S(2)}) collective-permute-start(bf16[128,1024]{1,0:T(8,128)(2,1)S(1)} %collective-permute-done.2), channel_id=1, source_target_pairs={{0,16},{8,24},{16,32},{24,40},{32,48},{40,56},{48,64},{56,72},{64,... | collective-permute-start | bytes 786440 | tf_op jit(solution)/shard_map/ppermute | solution.py:311
  43.9 13.5 %collective-permute-start.5 = (bf16[128,1024]{1,0:T(8,128)(2,1)S(1)}, bf16[128,1024]{1,0:T(8,128)(2,1)S(1)}, u32[]{:S(2)}, u32[]{:S(2)}) collective-permute-start(bf16[128,1024]{1,0:T(8,128)(2,1)S(1)} %collective-permute-done.3), channel_id=1, source_target_pairs={{0,112},{8,120},{16,0},{24,8},{32,16},{40,24},{48,32},{56,40},{64,... | collective-permute-start | bytes 786440 | tf_op jit(solution)/shard_map/ppermute | solution.py:311
  46.5 25.6 %collective-permute-start.9 = (bf16[256,1024]{1,0:T(8,128)(2,1)S(1)}, bf16[256,1024]{1,0:T(8,128)(2,1)S(1)}, u32[]{:S(2)}, u32[]{:S(2)}) collective-permute-start(bf16[256,1024]{1,0:T(8,128)(2,1)S(1)} %constant_dynamic-update-slice_fusion.refs_1_), channel_id=1, source_target_pairs={{0,8},{8,0},{16,24},{24,16},{32,40},{40,32},{48,56},{56,48},{64,72... | collective-permute-start | bytes 1572872 | tf_op jit(solution)/shard_map/ppermute | solution.py:312
  57.4 10.9 %collective-permute-start.7 = (bf16[64,1024]{1,0:T(8,128)(2,1)S(1)}, bf16[64,1024]{1,0:T(8,128)(2,1)S(1)}, u32[]{:S(2)}, u32[]{:S(2)}) collective-permute-start(bf16[64,1024]{1,0:T(8,128)(2,1)S(1)} %slice.70), channel_id=1, source_target_pairs={{0,112},{8,120},{16,0},{24,8},{32,16},{40,24},{48,32},{56,40},{64,... | collective-permute-start | bytes 393224 | tf_op jit(solution)/shard_map/ppermute | solution.py:311
  62.4 9.8 %collective-permute-start.10 = (bf16[256,1024]{1,0:T(8,128)(2,1)S(1)}, bf16[256,1024]{1,0:T(8,128)(2,1)S(1)}, u32[]{:S(2)}, u32[]{:S(2)}) collective-permute-start(bf16[256,1024]{1,0:T(8,128)(2,1)S(1)} %constant_dynamic-update-slice_fusion.2.refs_2_), channel_id=1, source_target_pairs={{0,8},{8,0},{16,24},{24,16},{32,40},{40,32},{48,56},{56,48},{64,72... | collective-permute-start | bytes 1572872 | tf_op jit(solution)/shard_map/ppermute | solution.py:312
  86.3 27.5 %all-to-all-start.1 = ((bf16[16,12,16,128]{3,2,1,0:T(8,128)(2,1)}), bf16[16,12,16,128]{3,2,1,0:T(8,128)(2,1)S(1)}, u32[]{:S(2)}, u32[]{:S(2)}) async-start(bf16[16,12,16,128]{3,2,1,0:T(8,128)(2,1)} %bitcast.8), calls=%async_computation.1 | async-start | bytes 1572864 | tf_op jit(solution)/shard_map/all_to_all | solution.py:288
  91.1 24.1 %collective-permute-start.27 = (bf16[32,16,128]{2,1,0:T(8,128)(2,1)S(1)}, bf16[32,16,128]{2,1,0:T(8,128)(2,1)S(1)}, u32[]{:S(2)}, u32[]{:S(2)}) collective-permute-start(bf16[32,16,128]{2,1,0:T(8,128)(2,1)S(1)} %get-tuple-element.19), channel_id=1, source_target_pairs={{0,7},{1,2},{2,1},{3,4},{4,3},{5,6},{6,5},{7,0},{8,15},{9,10},{10,... | collective-permute-start | bytes 393224 | tf_op jit(solution)/shard_map/ppermute | solution.py:284
  91.1 25.9 %collective-permute-start.28 = (bf16[32,16,128]{2,1,0:T(8,128)(2,1)S(1)}, bf16[32,16,128]{2,1,0:T(8,128)(2,1)S(1)}, u32[]{:S(2)}, u32[]{:S(2)}) collective-permute-start(bf16[32,16,128]{2,1,0:T(8,128)(2,1)S(1)} %get-tuple-element.20), channel_id=1, source_target_pairs={{0,2},{1,7},{2,4},{3,1},{4,6},{5,3},{6,0},{7,5},{8,10},{9,15},{10,... | collective-permute-start | bytes 393224 | tf_op jit(solution)/shard_map/ppermute | solution.py:284
  92.3 24.8 %collective-permute-start.29 = (bf16[32,16,128]{2,1,0:T(8,128)(2,1)S(1)}, bf16[32,16,128]{2,1,0:T(8,128)(2,1)S(1)}, u32[]{:S(2)}, u32[]{:S(2)}) collective-permute-start(bf16[32,16,128]{2,1,0:T(8,128)(2,1)S(1)} %get-tuple-element.21), channel_id=1, source_target_pairs={{0,5},{1,4},{2,7},{3,6},{4,1},{5,0},{6,3},{7,2},{8,13},{9,12},{10,... | collective-permute-start | bytes 393224 | tf_op jit(solution)/shard_map/ppermute | solution.py:284
  113.9 16.2 %collective-permute-start.16 = (bf16[48,16,128]{2,1,0:T(8,128)(2,1)S(1)}, bf16[48,16,128]{2,1,0:T(8,128)(2,1)S(1)}, u32[]{:S(2)}, u32[]{:S(2)}) collective-permute-start(bf16[48,16,128]{2,1,0:T(8,128)(2,1)S(1)} %bitcast.71), channel_id=1, source_target_pairs={{0,7},{1,2},{2,1},{3,4},{4,3},{5,6},{6,5},{7,0},{8,15},{9,10},{10,... | collective-permute-start | bytes 589832 | tf_op jit(solution)/shard_map/ppermute | solution.py:284
  114.0 16.1 %collective-permute-start.17 = (bf16[48,16,128]{2,1,0:T(8,128)(2,1)S(1)}, bf16[48,16,128]{2,1,0:T(8,128)(2,1)S(1)}, u32[]{:S(2)}, u32[]{:S(2)}) collective-permute-start(bf16[48,16,128]{2,1,0:T(8,128)(2,1)S(1)} %bitcast.70), channel_id=1, source_target_pairs={{0,2},{1,7},{2,4},{3,1},{4,6},{5,3},{6,0},{7,5},{8,10},{9,15},{10,... | collective-permute-start | bytes 589832 | tf_op jit(solution)/shard_map/ppermute | solution.py:284
  115.2 16.4 %collective-permute-start.18 = (bf16[48,16,128]{2,1,0:T(8,128)(2,1)S(1)}, bf16[48,16,128]{2,1,0:T(8,128)(2,1)S(1)}, u32[]{:S(2)}, u32[]{:S(2)}) collective-permute-start(bf16[48,16,128]{2,1,0:T(8,128)(2,1)S(1)} %bitcast.69), channel_id=1, source_target_pairs={{0,5},{1,4},{2,7},{3,6},{4,1},{5,0},{6,3},{7,2},{8,13},{9,12},{10,... | collective-permute-start | bytes 589832 | tf_op jit(solution)/shard_map/ppermute | solution.py:284
  118.0 34.3 %all-to-all-start.3 = ((bf16[16,8,16,128]{3,2,1,0:T(8,128)(2,1)}), bf16[16,8,16,128]{3,2,1,0:T(8,128)(2,1)S(1)}, u32[]{:S(2)}, u32[]{:S(2)}) async-start(bf16[16,8,16,128]{3,2,1,0:T(8,128)(2,1)} %bitcast.24), calls=%async_computation.3 | async-start | bytes 1048576 | tf_op jit(solution)/shard_map/all_to_all | solution.py:288
  121.9 11.8 %collective-permute-start.19 = (bf16[48,16,128]{2,1,0:T(8,128)(2,1)S(1)}, bf16[48,16,128]{2,1,0:T(8,128)(2,1)S(1)}, u32[]{:S(2)}, u32[]{:S(2)}) collective-permute-start(bf16[48,16,128]{2,1,0:T(8,128)(2,1)S(1)} %bitcast.60), channel_id=1, source_target_pairs={{0,1},{1,0},{2,3},{3,2},{4,5},{5,4},{6,7},{7,6},{8,9},{9,8},{10,11... | collective-permute-start | bytes 589832 | tf_op jit(solution)/shard_map/ppermute | solution.py:281
  130.1 11.1 %collective-permute-start.21 = (bf16[48,16,128]{2,1,0:T(8,128)(2,1)S(1)}, bf16[48,16,128]{2,1,0:T(8,128)(2,1)S(1)}, u32[]{:S(2)}, u32[]{:S(2)}) collective-permute-start(bf16[48,16,128]{2,1,0:T(8,128)(2,1)S(1)} %collective-permute-done.17.refs_2_), channel_id=1, source_target_pairs={{0,1},{1,0},{2,3},{3,2},{4,5},{5,4},{6,7},{7,6},{8,9},{9,8},{10,11... | collective-permute-start | bytes 589832 | tf_op jit(solution)/shard_map/ppermute | solution.py:281
  131.6 12.7 %collective-permute-start.22 = (bf16[48,16,128]{2,1,0:T(8,128)(2,1)S(1)}, bf16[48,16,128]{2,1,0:T(8,128)(2,1)S(1)}, u32[]{:S(2)}, u32[]{:S(2)}) collective-permute-start(bf16[48,16,128]{2,1,0:T(8,128)(2,1)S(1)} %collective-permute-done.18.refs_3_), channel_id=1, source_target_pairs={{0,1},{1,0},{2,3},{3,2},{4,5},{5,4},{6,7},{7,6},{8,9},{9,8},{10,11... | collective-permute-start | bytes 589832 | tf_op jit(solution)/shard_map/ppermute | solution.py:281
  150.1 20.2 %collective-permute-start.23 = (bf16[192,16,128]{2,1,0:T(8,128)(2,1)S(1)}, bf16[192,16,128]{2,1,0:T(8,128)(2,1)}, u32[]{:S(2)}, u32[]{:S(2)}) collective-permute-start(bf16[192,16,128]{2,1,0:T(8,128)(2,1)S(1)} %shard_map.86), channel_id=1, source_target_pairs={{0,1},{1,0},{2,3},{3,2},{4,5},{5,4},{6,7},{7,6},{8,9},{9,8},{10,11... | collective-permute-start | bytes 2359304 | tf_op jit(solution)/shard_map/ppermute | solution.py:281
  152.2 29.3 %collective-permute-start.30 = (bf16[128,16,128]{2,1,0:T(8,128)(2,1)S(1)}, bf16[128,16,128]{2,1,0:T(8,128)(2,1)}, u32[]{:S(2)}, u32[]{:S(2)}) collective-permute-start(bf16[128,16,128]{2,1,0:T(8,128)(2,1)S(1)} %bitcast.57), channel_id=1, source_target_pairs={{0,1},{1,0},{2,3},{3,2},{4,5},{5,4},{6,7},{7,6},{8,9},{9,8},{10,11... | collective-permute-start | bytes 1572872 | tf_op jit(solution)/shard_map/ppermute | solution.py:281
  172.5 38.7 %all-to-all-start.2 = ((bf16[16,12,16,128]{3,2,1,0:T(8,128)(2,1)}), bf16[16,12,16,128]{3,2,1,0:T(8,128)(2,1)S(1)}, u32[]{:S(2)}, u32[]{:S(2)}) async-start(bf16[16,12,16,128]{3,2,1,0:T(8,128)(2,1)} %bitcast.14), calls=%async_computation.2 | async-start | bytes 1572864 | tf_op jit(solution)/shard_map/all_to_all | solution.py:288
  188.6 10.2 %collective-permute-start.32 = (bf16[96,16,128]{2,1,0:T(8,128)(2,1)S(1)}, bf16[96,16,128]{2,1,0:T(8,128)(2,1)S(1)}, u32[]{:S(2)}, u32[]{:S(2)}) collective-permute-start(bf16[96,16,128]{2,1,0:T(8,128)(2,1)S(1)} %get-tuple-element.25), channel_id=1, source_target_pairs={{0,1},{1,0},{2,3},{3,2},{4,5},{5,4},{6,7},{7,6},{8,9},{9,8},{10,11... | collective-permute-start | bytes 1179656 | tf_op jit(solution)/shard_map/ppermute | solution.py:281
  189.9 13.9 %collective-permute-start.31 = (bf16[32,16,128]{2,1,0:T(8,128)(2,1)S(1)}, bf16[32,16,128]{2,1,0:T(8,128)(2,1)S(1)}, u32[]{:S(2)}, u32[]{:S(2)}) collective-permute-start(bf16[32,16,128]{2,1,0:T(8,128)(2,1)S(1)} %get-tuple-element.23), channel_id=1, source_target_pairs={{0,1},{1,0},{2,3},{3,2},{4,5},{5,4},{6,7},{7,6},{8,9},{9,8},{10,11... | collective-permute-start | bytes 393224 | tf_op jit(solution)/shard_map/ppermute | solution.py:281
  200.7 9.5 %collective-permute-start.35 = (bf16[32,16,128]{2,1,0:T(8,128)(2,1)S(1)}, bf16[32,16,128]{2,1,0:T(8,128)(2,1)S(1)}, u32[]{:S(2)}, u32[]{:S(2)}) collective-permute-start(bf16[32,16,128]{2,1,0:T(8,128)(2,1)S(1)} %get-tuple-element.41), channel_id=1, source_target_pairs={{5,0},{4,1},{7,2},{6,3},{1,4},{0,5},{3,6},{2,7},{13,8},{12,9},{15,... | collective-permute-start | bytes 393224 | tf_op jit(solution)/shard_map/ppermute | solution.py:284
  211.2 27.4 %all-to-all-start.4 = ((bf16[16,8,16,128]{3,2,1,0:T(8,128)(2,1)}), bf16[16,8,16,128]{3,2,1,0:T(8,128)(2,1)S(1)}, u32[]{:S(2)}, u32[]{:S(2)}) async-start(bf16[16,8,16,128]{3,2,1,0:T(8,128)(2,1)} %bitcast.30), calls=%async_computation.4 | async-start | bytes 1048576 | tf_op jit(solution)/shard_map/all_to_all | solution.py:288
  221.4 17.1 %collective-permute-start.24 = (bf16[48,16,128]{2,1,0:T(8,128)(2,1)S(1)}, bf16[48,16,128]{2,1,0:T(8,128)(2,1)S(1)}, u32[]{:S(2)}, u32[]{:S(2)}) collective-permute-start(bf16[48,16,128]{2,1,0:T(8,128)(2,1)S(1)} %bitcast.74), channel_id=1, source_target_pairs={{7,0},{2,1},{1,2},{4,3},{3,4},{6,5},{5,6},{0,7},{15,8},{10,9},{9,1... | collective-permute-start | bytes 589832 | tf_op jit(solution)/shard_map/ppermute | solution.py:284
  222.9 15.7 %collective-permute-start.25 = (bf16[48,16,128]{2,1,0:T(8,128)(2,1)S(1)}, bf16[48,16,128]{2,1,0:T(8,128)(2,1)S(1)}, u32[]{:S(2)}, u32[]{:S(2)}) collective-permute-start(bf16[48,16,128]{2,1,0:T(8,128)(2,1)S(1)} %bitcast.73), channel_id=1, source_target_pairs={{2,0},{7,1},{4,2},{1,3},{6,4},{3,5},{0,6},{5,7},{10,8},{15,9},{12,... | collective-permute-start | bytes 589832 | tf_op jit(solution)/shard_map/ppermute | solution.py:284
  225.5 18.4 %collective-permute-start.26 = (bf16[48,16,128]{2,1,0:T(8,128)(2,1)S(1)}, bf16[48,16,128]{2,1,0:T(8,128)(2,1)S(1)}, u32[]{:S(2)}, u32[]{:S(2)}) collective-permute-start(bf16[48,16,128]{2,1,0:T(8,128)(2,1)S(1)} %bitcast.72), channel_id=1, source_target_pairs={{5,0},{4,1},{7,2},{6,3},{1,4},{0,5},{3,6},{2,7},{13,8},{12,9},{15,... | collective-permute-start | bytes 589832 | tf_op jit(solution)/shard_map/ppermute | solution.py:284
  (13 other events, 134.2 us)
